TPU v7x, 1024 devices: a whole 8x8x8 slice. The times are simulated.
1024 devices in a mesh: dp: 128 (over z, y, core), tensor: 8 (over x).
Axes of the slice: x: 8, y: 8, z: 8, core: 2. Of those that a mesh axis runs over, the one named last changes fastest.
Arguments:
- grads: bfloat16 [128, 2, 4096, 1024], P('dp', None, None, 'tensor'), may hold values from -480 to 480
- master: float32 [2, 4096, 1024], P(None, 'dp', 'tensor'), may hold values from -0.09375 to 0.09375
- moment: float32 [2, 4096, 1024], P(None, 'dp', 'tensor'), may hold values from -0.06 to 0.06
- v_heads: float32 [8], P('tensor'), may hold values from 0.0001 to 0.001
- v_neurons: float32 [1024], P('tensor'), may hold values from 0.0001 to 0.001
Outputs:
- params: bfloat16 [2, 4096, 1024], P(None, None, 'tensor')
- new_master: float32 [2, 4096, 1024], P(None, 'dp', 'tensor')
- new_moment: float32 [2, 4096, 1024], P(None, 'dp', 'tensor')
- new_heads: float32 [8], P('tensor')
- new_neurons: float32 [1024], P('tensor')
All inputs are finite; a program needn't handle non-finite values.
Results may differ from a plain program's by a relative error of at most 0.001.
Values may be sent and summed in bfloat16 or wider, within the bound.
No kernel may reach another device: no remote copies, remote signals or barrier semaphores. Data moves between devices by JAX's collectives and lax.ppermute only.
A program may use at most 32 MiB of HBM per device.

v0:
```python
import jax
import jax.numpy as jnp
from jax import lax
from jax.sharding import Mesh
from jax.sharding import PartitionSpec as P

DIN = 4096
HEAD = 128
STEP = 2
DP = ("dp_0", "dp_1", "dp_2")


def own_block(pieces, axes, order):
    inside = pieces.shape[1:]
    pieces = pieces.reshape(*(lax.axis_size(a) for a in axes), *inside)
    pieces = jnp.moveaxis(pieces, order, range(len(axes))).reshape(-1, *inside)
    for k in order:
        pieces = lax.psum_scatter(pieces, axes[k], scatter_dimension=0, tiled=True)
    return pieces[0]


def in_blocks(shard, dim, size):
    shape = shard.shape
    pieces = shard.reshape(*shape[:dim], size, shape[dim] // size, *shape[dim + 1 :])
    return jnp.moveaxis(pieces, dim, 0)


def summed_rows(shard, axes, order, dim):
    size = lax.axis_size(axes)
    return own_block(in_blocks(shard, dim, size), axes, order)


def over_axes(shard, axes):
    for axis in axes:
        shard = lax.psum(shard, axis)
    return shard


def copy_for_each(shard, axis):
    copies = jnp.broadcast_to(shard, (lax.axis_size(axis), *shard.shape))
    return lax.all_to_all(copies, axis, split_axis=0, concat_axis=0, tiled=True)


def of_everyone(shard, axis):
    everything = copy_for_each(shard, axis)
    return jnp.sum(everything, axis=0)


def on_device(grads, master, moment, v_heads, v_neurons):
    replicas = lax.axis_size(DP)
    terms = grads[0].astype(jnp.float32)
    local_heads = v_heads.shape[0]
    summed = summed_rows(terms, DP, (2, 0, 1), 1)
    gradient = summed / replicas
    key_rows = gradient[0].reshape(gradient.shape[1], local_heads, HEAD)
    heads_local = jnp.sum(key_rows * key_rows, axis=(0, 2))
    neurons_local = jnp.sum(gradient[1] * gradient[1], axis=0)
    head_sq, neuron_sq = (over_axes(heads_local, DP), over_axes(neurons_local, DP))
    total = of_everyone(jnp.sum(head_sq) + jnp.sum(neuron_sq), "tensor")
    clip = jnp.minimum(1.0, 256.0 / (jnp.sqrt(total) + 1e-06))
    new_moment = 0.9 * moment + 0.1 * clip * gradient
    new_heads = 0.95 * v_heads + 0.05 * clip * clip * head_sq / (DIN * HEAD)
    new_neurons = 0.95 * v_neurons + 0.05 * clip * clip * neuron_sq / DIN
    second_fix = 1.0 - 0.95**STEP
    first_fix = 1.0 - 0.9**STEP
    key_denom = jnp.repeat(jnp.sqrt(new_heads / second_fix) + 1e-08, HEAD)
    value_denom = jnp.sqrt(new_neurons / second_fix) + 1e-08
    denom = jnp.stack([key_denom, value_denom])
    update = new_moment / first_fix / denom[:, None, :]
    new_master = master - 0.01 * (update + 0.1 * master)
    shard_params = new_master.astype(jnp.bfloat16)
    params = lax.all_gather(shard_params, DP, axis=1, tiled=True)
    return (params, new_master, new_moment, new_heads, new_neurons)


def solution(mesh):
    split = Mesh(
        mesh.devices.reshape(8, 8, 2, mesh.shape["tensor"]), ("dp_0", "dp_1", "dp_2", "tensor")
    )
    return jax.shard_map(
        on_device,
        mesh=split,
        in_specs=(
            P(DP, None, None, "tensor"),
            P(None, DP, "tensor"),
            P(None, DP, "tensor"),
            P("tensor"),
            P("tensor"),
        ),
        out_specs=(
            P(None, None, "tensor"),
            P(None, DP, "tensor"),
            P(None, DP, "tensor"),
            P("tensor"),
            P("tensor"),
        ),
        check_vma=False,
    )
```

profile of v0, /device:TPU:1, one launch (start us, length us, event | category | flops | bytes accessed | tf_op | source)
XLA Modules:
  0.0 297.9 jit_solution(2110349624676879648)
XLA Ops:
  7.2 0.0 reduce-scatter.4.cloned.1.call-start
  7.2 2.2 convert.5
  9.4 2.6 copy.15
  12.0 0.0 reduce-scatter.4.cloned.1.call-update
  12.0 0.0 copy-start.2
  12.0 0.0 copy-start
  12.0 0.0 copy-start.1
  12.0 0.0 reduce-scatter.6.cloned.1.call-start
  12.1 37.4 %reduce-scatter.4.cloned.1.call-done = f32[64,2,32,128]{3,2,1,0:T(8,128)} async-done(((f32[128,2,32,128]{3,2,1,0:T(8,128)}), f32[64,2,32,128]{3,2,1,0:T(8,128)}) %reduce-scatter.4.cloned.1.call-update) | async-done | bytes 2097168 | tf_op jit(solution)/shard_map/reduce_scatter | solution.py:18
  49.5 0.0 reduce-scatter.6.cloned.1.call-update
  49.5 0.0 reduce-scatter.8.cloned.1.call-start
  49.6 48.5 %reduce-scatter.6.cloned.1.call-done = f32[8,2,32,128]{3,2,1,0:T(8,128)} async-done(((f32[64,2,32,128]{3,2,1,0:T(8,128)}), f32[8,2,32,128]{3,2,1,0:T(8,128)}) %reduce-scatter.6.cloned.1.call-update) | async-done | bytes 262160 | tf_op jit(solution)/shard_map/reduce_scatter | solution.py:18
  98.1 0.0 reduce-scatter.8.cloned.1.call-update
  98.8 41.6 %reduce-scatter.8.cloned.1.call-done = f32[1,2,32,128]{3,2,1,0:T(8,128)} async-done(((f32[8,2,32,128]{3,2,1,0:T(8,128)}), f32[1,2,32,128]{3,2,1,0:T(8,128)}) %reduce-scatter.8.cloned.1.call-update) | async-done | bytes 32784 | tf_op jit(solution)/shard_map/reduce_scatter | solution.py:18
  140.4 0.8 broadcast_multiply_fusion
  141.1 0.6 fusion
  141.7 16.0 %all-reduce.2 = (f32[1]{0:T(128)}, f32[128]{0:T(128)S(1)}) all-reduce(f32[1]{0:T(128)} %bitcast.6, f32[128]{0:T(128)S(1)} %get-tuple-element.5), channel_id=1, replica_groups=mesh['dp_0'=8,'dp_1'=8,'dp_2'=2,'tensor'=8] {'dp_0'}, use_global_device_ids=true, to_apply=%region_4.0 | all-reduce | flops 129 | bytes 1032 | tf_op jit(solution)/shard_map/psum | solution.py:35
  157.8 12.6 %all-reduce.1 = (f32[1]{0:T(128)}, f32[128]{0:T(128)S(1)}) all-reduce(f32[1]{0:T(128)} %get-tuple-element.9, f32[128]{0:T(128)S(1)} %get-tuple-element.10), channel_id=1, replica_groups=mesh['dp_0'=8,'dp_1'=8,'dp_2'=2,'tensor'=8] {'dp_1'}, use_global_device_ids=true, to_apply=%region_5.0 | all-reduce | flops 129 | bytes 1032 | tf_op jit(solution)/shard_map/psum | solution.py:35
  170.4 16.2 %all-reduce.3 = (f32[1]{0:T(128)}, f32[128]{0:T(128)S(1)}) all-reduce(f32[1]{0:T(128)} %get-tuple-element.7, f32[128]{0:T(128)S(1)} %get-tuple-element.8), channel_id=1, replica_groups=mesh['dp_0'=8,'dp_1'=8,'dp_2'=2,'tensor'=8] {'dp_2'}, use_global_device_ids=true, to_apply=%region_6.0 | all-reduce | flops 129 | bytes 1032 | tf_op jit(solution)/shard_map/psum | solution.py:35
  186.7 0.6 reduce_sum.48
  188.6 0.6 broadcast_in_dim.2
  189.1 6.4 %all-to-all-start = ((f32[8,1,1]{2,1,0:T(1,128)}), f32[8,1,1]{2,1,0:T(1,128)S(1)}, u32[]{:S(2)}, u32[]{:S(2)}) async-start(f32[8,1,1]{2,1,0:T(1,128)} %broadcast_in_dim.2), calls=%async_computation.3 | async-start | bytes 8192 | tf_op jit(solution)/shard_map/all_to_all | solution.py:41
  195.5 0.0 all-gather.2.cloned.1.call-start
  195.6 6.4 %all-to-all-done = f32[8,1,1]{2,1,0:T(1,128)S(1)} async-done(((f32[8,1,1]{2,1,0:T(1,128)}), f32[8,1,1]{2,1,0:T(1,128)S(1)}, u32[]{:S(2)}, u32[]{:S(2)}) %all-to-all-start) | async-done | bytes 64 | tf_op jit(solution)/shard_map/all_to_all | solution.py:41
  202.0 0.6 reduce_sum.49
  204.1 0.0 copy-done.2
  204.1 0.5 add_bitcast_fusion
  204.6 0.0 copy-done
  204.6 0.0 copy-done.1
  204.6 1.4 fusion.2
  206.0 0.0 all-gather.2.cloned.1.call-update
  206.0 81.2 %all-gather.2.cloned.1.call-done = bf16[2,4096,128]{2,1,0:T(8,128)(2,1)} async-done(((bf16[2,32,128]{2,1,0:T(8,128)(2,1)}), bf16[2,4096,128]{2,1,0:T(8,128)(2,1)}) %all-gather.2.cloned.1.call-update) | async-done | bytes 2097168 | tf_op jit(solution)/shard_map/all_gather | solution.py:72
  287.2 3.0 %copy.21 = bf16[2,4096,128]{2,1,0:T(8,128)(2,1)} copy(bf16[2,4096,128]{2,1,0:T(8,128)(2,1)} %all-gather.2.cloned.1.call-done) | data formatting | bytes 4194304
  (1 shorter events, 0.0 us)
Async XLA Ops:
  7.2 42.3 %reduce-scatter.4.cloned.1.call-start = ((), (), s32[]{:S(2)}) async-start(), calls=%async_computation.4 | async-start | bytes 6291456 | tf_op jit(solution)/shard_map/reduce_scatter | solution.py:18
  12.0 192.1 %copy-start.2 = (f32[128]{0:T(128)S(1)}, f32[128]{0:T(128)}, u32[]{:S(2)}) copy-start(f32[128]{0:T(128)} %param.9) | copy-start | bytes 1540
  12.0 192.6 %copy-start = (f32[2,32,128]{2,1,0:T(8,128)S(1)}, f32[2,32,128]{2,1,0:T(8,128)}, u32[]{:S(2)}) copy-start(f32[2,32,128]{2,1,0:T(8,128)} %param.6) | copy-start | bytes 98308
  12.0 192.6 %copy-start.1 = (f32[2,32,128]{2,1,0:T(8,128)S(1)}, f32[2,32,128]{2,1,0:T(8,128)}, u32[]{:S(2)}) copy-start(f32[2,32,128]{2,1,0:T(8,128)} %param.7) | copy-start | bytes 98308
  12.0 86.1 %reduce-scatter.6.cloned.1.call-start = ((), (), s32[]{:S(2)}) async-start(), calls=%async_computation.5 | async-start | bytes 2359296 | tf_op jit(solution)/shard_map/reduce_scatter | solution.py:18
  49.5 90.8 %reduce-scatter.8.cloned.1.call-start = ((), (), s32[]{:S(2)}) async-start(), calls=%async_computation.6 | async-start | bytes 294912 | tf_op jit(solution)/shard_map/reduce_scatter | solution.py:18
  189.1 12.9 %all-to-all-start = ((f32[8,1,1]{2,1,0:T(1,128)}), f32[8,1,1]{2,1,0:T(1,128)S(1)}, u32[]{:S(2)}, u32[]{:S(2)}) async-start(f32[8,1,1]{2,1,0:T(1,128)} %broadcast_in_dim.2), calls=%async_computation.3 | async-start | bytes 8192 | tf_op jit(solution)/shard_map/all_to_all | solution.py:41
  195.5 91.7 %all-gather.2.cloned.1.call-start = ((), (), s32[]{:S(2)}) async-start(), calls=%async_computation.7 | async-start | bytes 2113536 | tf_op jit(solution)/shard_map/all_gather | solution.py:72
Sparse Core Ops, SparseCore 0:
  12.1 37.3 reduce-scatter.3
  52.9 45.1 reduce-scatter.5
  101.5 38.8 reduce-scatter.7
  206.2 81.0 all-gather.1
where the time goes:
time: 298 us
  waiting for transfers between devices  215 us (72%)
  blocking collectives  44.9 us (15%)
  between operations  18.3 us (6%)
  other arithmetic  6.67 us (2%)
  starting transfers between devices  6.55 us (2%)
  local copies, waits for them, and re-layouts  6.24 us (2%)
    reduce_scatter x3, waiting for transfers between devices, own_block(): pieces = lax.psum_scatter(pieces, axes[k], scatter_dimension=0, tiled=True)  128 us
    all_gather x1, waiting for transfers between devices, on_device(): params = lax.all_gather(shard_params, DP, axis=1, tiled=True)  81.2 us
    psum x3, blocking collectives, over_axes(): shard = lax.psum(shard, axis)  44.9 us
    all_to_all x1, waiting for transfers between devices, copy_for_each(): return lax.all_to_all(copies, axis, split_axis=0, concat_axis=0, tiled=True)  6.44 us
    all_to_all x1, starting transfers between devices, copy_for_each(): return lax.all_to_all(copies, axis, split_axis=0, concat_axis=0, tiled=True)  6.4 us
  transfers between devices with their start and end apart: 5, of which 5 were waited for; matrix products, arithmetic and copies ran while one was open for 0% of the time, Pallas kernels for 0%

commit v1 on v0

v1 whole, which is shorter than its diff:
```python
import functools

import jax
import jax.numpy as jnp
from jax import lax
from jax.experimental import pallas as pl
from jax.experimental.pallas import tpu as pltpu
from jax.sharding import Mesh
from jax.sharding import PartitionSpec as P

DIN = 4096
HEAD = 128
STEP = 2
DP = ("z", "y", "c")
NZ, NY, NC, NX = 8, 8, 2, 8
ROWS = 32
SECOND_FIX = 1.0 - 0.95**STEP
FIRST_FIX = 1.0 - 0.9**STEP


def flat(z, y, c):
    return (z * NY + y) * NC + c


ALONG_Z = [[flat(z, y, c) for z in range(NZ)] for y in range(NY) for c in range(NC)]
Z_THEN_Y = [[flat(z, y, 0) for z in range(NZ)] for y in range(NY)] + [
    [flat(z, y, 1) for y in range(NY)] for z in range(NZ)
]
Y_THEN_Z = [[flat(z, y, 0) for y in range(NY)] for z in range(NZ)] + [
    [flat(z, y, 1) for z in range(NZ)] for y in range(NY)
]


def exchange(blocks, axes, groups=None):
    return lax.all_to_all(blocks, axes, split_axis=0, concat_axis=0, tiled=True, axis_index_groups=groups)


def swap_cores(x):
    return lax.ppermute(x, "c", [(0, 1), (1, 0)])


def pair_sum_kernel(core_ref, mine_ref, got_ref, out_ref, power_ref):
    core = core_ref[0]

    def add(i, top):
        hi, lo = i // 8, i % 8
        source = jnp.where(core == 0, i, lo * 8 + hi)
        for p in range(2):
            total = mine_ref[p, source].astype(jnp.float32) + got_ref[p, source].astype(jnp.float32)
            out_ref[i, p] = total
            top = jnp.maximum(top, jnp.max(jnp.abs(total).reshape(4, 8, 128), axis=0))
        return top

    top = lax.fori_loop(0, 64, add, jnp.zeros((8, 128), jnp.float32), unroll=4)
    largest = jnp.max(jnp.max(top, axis=0, keepdims=True), axis=1, keepdims=True)
    power = jnp.floor(jnp.log2(jnp.maximum(jnp.broadcast_to(largest, (8, 128)), 2.0**-100)))
    power_ref[...] = power
    scale = jnp.exp2(14.0 - power)[:1]

    def rescale(i, carry):
        for p in range(2):
            out_ref[i, p] = out_ref[i, p] * scale
        return carry

    lax.fori_loop(0, 64, rescale, 0, unroll=4)


def pair_sum(core, mine, got):
    vmem = pl.BlockSpec(memory_space=pltpu.VMEM)
    return pl.pallas_call(
        pair_sum_kernel,
        in_specs=[pl.BlockSpec(memory_space=pltpu.SMEM), vmem, vmem],
        out_specs=[vmem, vmem],
        out_shape=[
            jax.ShapeDtypeStruct((64, 2, ROWS, HEAD), jnp.float32),
            jax.ShapeDtypeStruct((8, HEAD), jnp.float32),
        ],
        name="pair_sum",
    )(core, mine, got)


def gradient_kernel(parts_ref, gradient_ref, send_ref):
    total = parts_ref[0]
    for k in range(1, 8):
        total = total + parts_ref[k]
    gradient = total / 128.0
    gradient_ref[...] = gradient
    squares = gradient * gradient
    head = jnp.sum(jnp.sum(squares[0], axis=0, keepdims=True), axis=1, keepdims=True)
    send_ref[:, 0:1, :] = jnp.broadcast_to(jnp.sum(squares[1], axis=0, keepdims=True)[None], (16, 1, HEAD))
    send_ref[:, 1:2, :] = jnp.broadcast_to(head[None], (16, 1, HEAD))


def gradient_of(parts):
    vmem = pl.BlockSpec(memory_space=pltpu.VMEM)
    return pl.pallas_call(
        gradient_kernel,
        in_specs=[vmem],
        out_specs=[vmem, vmem],
        out_shape=[
            jax.ShapeDtypeStruct((2, ROWS, HEAD), jnp.float32),
            jax.ShapeDtypeStruct((16, 2, HEAD), jnp.float32),
        ],
        name="gradient",
    )(parts)


def chip_stats_kernel(x_ref, got_ref, send_ref):
    x = x_ref[0]
    everyone = jnp.sum(got_ref[...], axis=0)
    lane = lax.broadcasted_iota(jnp.int32, (1, HEAD), 1)
    total = jnp.sum(everyone[0:1], axis=1, keepdims=True) + everyone[1:2]
    mine = got_ref[x] + got_ref[x + NX]
    send_ref[:, 0:1, :] = jnp.broadcast_to(mine[0:1][None], (64, 1, HEAD))
    send_ref[:, 1:2, :] = jnp.broadcast_to(jnp.where(lane == 0, mine[1:2], total)[None], (64, 1, HEAD))


def chip_stats(x, got):
    vmem = pl.BlockSpec(memory_space=pltpu.VMEM)
    return pl.pallas_call(
        chip_stats_kernel,
        in_specs=[pl.BlockSpec(memory_space=pltpu.SMEM), vmem],
        out_specs=vmem,
        out_shape=jax.ShapeDtypeStruct((64, 2, HEAD), jnp.float32),
        name="chip_stats",
    )(x, got)


def update_kernel(stats_ref, gradient_ref, master_ref, moment_ref, heads_ref, neurons_ref,
                  send_ref, new_master_ref, new_moment_ref, new_heads_ref, new_neurons_ref):
    stats = jnp.sum(stats_ref[...], axis=0)
    neuron_sq, other = stats[0:1], stats[1:2]
    lane = lax.broadcasted_iota(jnp.int32, (1, HEAD), 1)
    head_sq = jnp.sum(jnp.where(lane == 0, other, 0.0), axis=1, keepdims=True)
    total = jnp.sum(jnp.where(lane == 1, other, 0.0), axis=1, keepdims=True)
    clip = jnp.minimum(1.0, 256.0 / (jnp.sqrt(jnp.broadcast_to(total, (1, HEAD))) + 1e-06))
    new_heads = 0.95 * heads_ref[...] + 0.05 * clip * clip * head_sq / (DIN * HEAD)
    new_neurons = 0.95 * neurons_ref[...] + 0.05 * clip * clip * neuron_sq / DIN
    new_heads_ref[...] = new_heads
    new_neurons_ref[...] = new_neurons
    for p, second in ((0, new_heads), (1, new_neurons)):
        denom = jnp.sqrt(second / SECOND_FIX) + 1e-08
        new_moment = 0.9 * moment_ref[p] + 0.1 * clip * gradient_ref[p]
        update = new_moment / FIRST_FIX / denom
        master = master_ref[p]
        new_master = master - 0.01 * (update + 0.1 * master)
        new_moment_ref[p] = new_moment
        new_master_ref[p] = new_master
        params = new_master.astype(jnp.bfloat16)
        for k in range(8):
            send_ref[k, p] = params


def update_of(stats, gradient, master, moment, heads, neurons):
    vmem = pl.BlockSpec(memory_space=pltpu.VMEM)
    own = jax.ShapeDtypeStruct((2, ROWS, HEAD), jnp.float32)
    row = jax.ShapeDtypeStruct((1, HEAD), jnp.float32)
    return pl.pallas_call(
        update_kernel,
        in_specs=[vmem] * 6,
        out_specs=[vmem] * 5,
        out_shape=[jax.ShapeDtypeStruct((8, 2, ROWS, HEAD), jnp.bfloat16), own, own, row, row],
        name="update",
    )(stats, gradient, master, moment, heads, neurons)


def assemble_kernel(core_ref, mine_ref, got_ref, out_ref):
    core = core_ref[0]

    def place(i, carry):
        hi, lo = i // 8, i % 8
        turned = lo * 8 + hi
        for p in range(2):
            out_ref[p, jnp.where(core == 0, i, turned), core] = mine_ref[i, p]
            out_ref[p, jnp.where(core == 0, turned, i), 1 - core] = got_ref[i, p]
        return carry

    lax.fori_loop(0, 64, place, 0, unroll=4)


def assemble(core, mine, got):
    vmem = pl.BlockSpec(memory_space=pltpu.VMEM)
    return pl.pallas_call(
        assemble_kernel,
        in_specs=[pl.BlockSpec(memory_space=pltpu.SMEM), vmem, vmem],
        out_specs=vmem,
        out_shape=jax.ShapeDtypeStruct((2, 64, 2, ROWS, HEAD), jnp.bfloat16),
        name="assemble",
    )(core, mine, got)


def on_device(grads, master, moment, v_heads, v_neurons):
    c = lax.axis_index("c")
    core = c.reshape(1).astype(jnp.int32)
    x = lax.axis_index("x").reshape(1).astype(jnp.int32)

    halves = grads[0].reshape(2, 64, 2, ROWS, HEAD)
    theirs = lax.dynamic_index_in_dim(halves, 1 - c, 2, keepdims=False)
    mine = lax.dynamic_index_in_dim(halves, c, 2, keepdims=False)
    sums, power = pair_sum(core, mine, swap_cores(theirs))

    message = jnp.concatenate(
        [
            sums.reshape(8, 512, HEAD).astype(jnp.float16),
            jnp.broadcast_to(power.astype(jnp.float16), (8, 8, HEAD)),
        ],
        axis=1,
    )
    got = exchange(message, DP, Z_THEN_Y)
    scale = jnp.exp2(got[:, 512, 0].astype(jnp.float32) - 14.0)
    partial = jnp.sum(got[:, :512].astype(jnp.float32) * scale[:, None, None], axis=0)
    parts = exchange(partial.reshape(8, 2 * ROWS, HEAD), DP, Y_THEN_Z)

    gradient, send = gradient_of(parts.reshape(8, 2, ROWS, HEAD))
    send = chip_stats(x, exchange(send, ("c", "x")))
    stats = exchange(send, DP, [[flat(z, y, k) for z in range(NZ) for y in range(NY)] for k in range(NC)])

    heads = jnp.broadcast_to(v_heads, (1, HEAD))
    copies, new_master, new_moment, new_heads, new_neurons = update_of(
        stats, gradient, master, moment, heads, v_neurons.reshape(1, HEAD)
    )
    line = exchange(copies.reshape(8, 2 * ROWS, HEAD), DP, Y_THEN_Z)
    plane = exchange(jnp.broadcast_to(line.reshape(1, 512, HEAD), (8, 512, HEAD)), DP, Z_THEN_Y)
    plane = plane.reshape(64, 2, ROWS, HEAD)
    params = assemble(core, plane, swap_cores(plane)).reshape(2, DIN, HEAD)
    return (params, new_master, new_moment, new_heads[0, :1], new_neurons.reshape(HEAD))


def solution(mesh):
    split = Mesh(mesh.devices.reshape(NZ, NY, NC, NX), ("z", "y", "c", "x"))
    return jax.shard_map(
        on_device,
        mesh=split,
        in_specs=(
            P(DP, None, None, "x"),
            P(None, DP, "x"),
            P(None, DP, "x"),
            P("x"),
            P("x"),
        ),
        out_specs=(
            P(None, None, "x"),
            P(None, DP, "x"),
            P(None, DP, "x"),
            P("x"),
            P("x"),
        ),
        check_vma=False,
    )
```

time: 298 us -> 151 us (0.51)
  waiting for transfers between devices: 215 us -> 22 us
  starting transfers between devices: 6.55 us -> 36.4 us
  blocking collectives: 44.9 us -> 69.7 us
  between operations: 18.3 us -> 1.37 us
  Pallas kernels: 0 us -> 12.1 us
  other arithmetic: 6.67 us -> 2.46 us
    reduce_scatter x3 -> x0, waiting for transfers between devices: 128 us -> none  [own_block(): pieces = lax.psum_scatter(pieces, axes[k], scatter_dimension=0, tiled=True)]
    all_gather x1 -> x0, waiting for transfers between devices: 81.2 us -> none  [on_device(): params = lax.all_gather(shard_params, DP, axis=1, tiled=True)]
    all_to_all x0 -> x4, blocking collectives: none -> 69.7 us  [exchange(): lax.all_to_all(blocks, axes, split_axis=0, concat_axis=0, tiled=True, axi...]
    psum x3 -> x0, blocking collectives: 44.9 us -> none  [over_axes(): shard = lax.psum(shard, axis)]
    ppermute x0 -> x2, starting transfers between devices: none -> 21.8 us  [swap_cores(): return lax.ppermute(x, 'c', [(0, 1), (1, 0)])]
    pallas_call x0 -> x5, Pallas kernels: none -> 12.1 us  [the longest x1 3.74 us: pair_sum(): pl.pallas_call(pair_sum_kernel, in_specs=[pl.BlockSpec(memory_space=pltpu...]
    all_to_all x1 -> x2, waiting for transfers between devices: 6.44 us -> 17.5 us  [exchange(): lax.all_to_all(blocks, axes, split_axis=0, concat_axis=0, tiled=True, axi...]
    all_to_all x1 -> x2, starting transfers between devices: 6.4 us -> 14.6 us  [exchange(): lax.all_to_all(blocks, axes, split_axis=0, concat_axis=0, tiled=True, axi...]
  transfers between devices with their start and end apart: 5 -> 4, of which waited for: 5 -> 4; matrix products, arithmetic and copies ran while one was open for 0% -> 0% of each run, Pallas kernels for 0% -> 0%
where the time goes in v1:
time: 151 us; the launch traced here: 150 us
  blocking collectives  69.7 us (46%)
  starting transfers between devices  36.4 us (24%)
  waiting for transfers between devices  22 us (15%)
  Pallas kernels  12.1 us (8%)
  local copies, waits for them, and re-layouts  6.44 us (4%)
  other arithmetic  2.46 us (2%)
    all_to_all x4, blocking collectives, exchange(): lax.all_to_all(blocks, axes, split_axis=0, concat_axis=0, tiled=True, axi...  69.7 us
    ppermute x2, starting transfers between devices, swap_cores(): return lax.ppermute(x, 'c', [(0, 1), (1, 0)])  21.8 us
    all_to_all x2, waiting for transfers between devices, exchange(): lax.all_to_all(blocks, axes, split_axis=0, concat_axis=0, tiled=True, axi...  17.5 us
    all_to_all x2, starting transfers between devices, exchange(): lax.all_to_all(blocks, axes, split_axis=0, concat_axis=0, tiled=True, axi...  14.6 us
    ppermute x2, waiting for transfers between devices, swap_cores(): return lax.ppermute(x, 'c', [(0, 1), (1, 0)])  4.53 us
    pallas_call x1, Pallas kernels, pair_sum(): pl.pallas_call(pair_sum_kernel, in_specs=[pl.BlockSpec(memory_space=pltpu...  3.74 us
    pallas_call x1, Pallas kernels, assemble(): pl.pallas_call(assemble_kernel, in_specs=[pl.BlockSpec(memory_space=pltpu...  3.49 us
  transfers between devices with their start and end apart: 4, of which 4 were waited for; matrix products, arithmetic and copies ran while one was open for 0% of the time, Pallas kernels for 0%

profile of v1, /device:TPU:1, one launch (start us, length us, event | category | flops | bytes accessed | tf_op | source)
XLA Modules:
  0.0 150.4 jit_solution(6595136208648526990)
XLA Ops:
  0.6 2.9 %dynamic-slice_bitcast_fusion = (bf16[2,64,32,128]{3,2,1,0:T(8,128)(2,1)S(1)}, bf16[2,64,32,128]{3,2,1,0:T(8,128)(2,1)}) fusion(bf16[2,64,2,32,128]{4,3,2,1,0:T(8,128)(2,1)} %bitcast.29, s32[]{:T(128)S(6)} %select_n.8, s32[]{:T(128)S(6)} %select_n.7), kind=kLoop, calls=%fused_computation.2 | loop fusion | bytes 4194312 | tf_op jit(solution)/shard_map/jit(dynamic_index_in_dim)/squeeze | solution.py:198
  3.6 16.0 %collective-permute-start = (bf16[2,64,32,128]{3,2,1,0:T(8,128)(2,1)S(1)}, bf16[2,64,32,128]{3,2,1,0:T(8,128)(2,1)S(1)}, u32[]{:S(2)}, u32[]{:S(2)}) collective-permute-start(bf16[2,64,32,128]{3,2,1,0:T(8,128)(2,1)S(1)} %get-tuple-element.23), channel_id=1, source_target_pairs={{0,8},{8,0},{1,9},{9,1},{2,10},{10,2},{3,11},{11,3},{4,12},{12,4},... | collective-permute-start | bytes 3145736 | tf_op jit(solution)/shard_map/ppermute | solution.py:39
  19.6 2.3 %collective-permute-done.got_ref = bf16[2,64,32,128]{3,2,1,0:T(8,128)(2,1)S(1)} collective-permute-done((bf16[2,64,32,128]{3,2,1,0:T(8,128)(2,1)S(1)}, bf16[2,64,32,128]{3,2,1,0:T(8,128)(2,1)S(1)}, u32[]{:S(2)}, u32[]{:S(2)}) %collective-permute-start) | collective-permute-done | bytes 1048608 | tf_op jit(solution)/shard_map/ppermute | solution.py:39
  21.9 0.0 copy-start.2
  21.9 1.0 copy-done.2
  22.9 3.7 %pair_sum.1 = (f32[64,2,32,128]{3,2,1,0:T(8,128)}, f32[8,128]{1,0:T(8,128)}) custom-call(s32[1]{0:T(128)} %bitcast.core_ref, bf16[2,64,32,128]{3,2,1,0:T(8,128)(2,1)} %get-tuple-element.24.mine_ref, bf16[2,64,32,128]{3,2,1,0:T(8,128)(2,1)} %copy-done.2), custom_call_target="tpu_custom_call" | custom-call | tf_op jit(solution)/shard_map/pair_sum/pallas_call | solution.py:70
  26.6 0.0 copy-start.5
  26.6 1.9 %convert_element_type.16 = f16[64,2,32,128]{3,2,1,0:T(8,128)(2,1)S(1)} convert(f32[64,2,32,128]{3,2,1,0:T(8,128)} %get-tuple-element.14) | non-fusion elementwise | flops 524288 | bytes 3145728 | tf_op jit(solution)/shard_map/convert_element_type | solution.py:204
  28.5 0.0 copy-done.5
  28.5 0.3 pad_maximum_fusion
  28.8 20.4 %all_to_all.30 = f16[8,520,128]{2,1,0:T(8,128)(2,1)S(1)} all-to-all(f16[8,520,128]{2,1,0:T(8,128)(2,1)S(1)} %pad_maximum_fusion), channel_id=1, replica_groups={{0,128,256,384,512,640,768,896},{16,144,272,400,528,656,784,912},{32,16..., dimensions={0} | all-to-all | bytes 2129920 | tf_op jit(solution)/shard_map/all_to_all | solution.py:35
  49.2 0.1 copy.22
  49.3 0.3 multiply_reduce_fusion
  49.6 17.7 %all_to_all.31 = f32[8,64,128]{2,1,0:T(8,128)} all-to-all(f32[8,64,128]{2,1,0:T(8,128)S(1)} %bitcast.31), channel_id=1, replica_groups={{0,16,32,48,64,80,96,112},{128,144,160,176,192,208,224,240},{256,272,28..., dimensions={0} | all-to-all | bytes 524288 | tf_op jit(solution)/shard_map/all_to_all | solution.py:35
  67.3 1.7 %gradient.1 = (f32[2,32,128]{2,1,0:T(8,128)}, f32[16,2,128]{2,1,0:T(2,128)}) custom-call(f32[8,2,32,128]{3,2,1,0:T(8,128)} %bitcast.32), custom_call_target="tpu_custom_call" | custom-call | tf_op jit(solution)/shard_map/gradient/pallas_call | solution.py:96
  68.9 10.0 %all-to-all-start.2 = ((f32[16,2,128]{2,1,0:T(2,128)}), f32[16,2,128]{2,1,0:T(2,128)S(1)}, u32[]{:S(2)}, u32[]{:S(2)}) async-start(f32[16,2,128]{2,1,0:T(2,128)} %get-tuple-element.16), calls=%async_computation.2 | async-start | bytes 32768 | tf_op jit(solution)/shard_map/all_to_all | solution.py:35
  78.9 7.0 %all-to-all-done.2.got_ref = f32[16,2,128]{2,1,0:T(2,128)S(1)} async-done(((f32[16,2,128]{2,1,0:T(2,128)}), f32[16,2,128]{2,1,0:T(2,128)S(1)}, u32[]{:S(2)}, u32[]{:S(2)}) %all-to-all-start.2) | async-done | bytes 16416 | tf_op jit(solution)/shard_map/all_to_all | solution.py:35
  85.9 0.0 copy-start.4
  85.9 0.6 copy-done.4
  86.6 1.5 chip_stats.1
  88.0 4.6 %all-to-all-start.3 = ((f32[64,2,128]{2,1,0:T(2,128)}), f32[64,2,128]{2,1,0:T(2,128)S(1)}, u32[]{:S(2)}, u32[]{:S(2)}) async-start(f32[64,2,128]{2,1,0:T(2,128)} %chip_stats.1), calls=%async_computation.3 | async-start | bytes 131072 | tf_op jit(solution)/shard_map/all_to_all | solution.py:35
  93.3 10.4 %all-to-all-done.3.stats_ref = f32[64,2,128]{2,1,0:T(2,128)S(1)} async-done(((f32[64,2,128]{2,1,0:T(2,128)}), f32[64,2,128]{2,1,0:T(2,128)S(1)}, u32[]{:S(2)}, u32[]{:S(2)}) %all-to-all-start.3) | async-done | bytes 65568 | tf_op jit(solution)/shard_map/all_to_all | solution.py:35
  103.7 0.0 copy-start.3
  103.7 0.5 broadcast_in_dim.17.heads_ref
  104.2 0.1 copy-done.3
  104.3 1.8 %update.1 = (bf16[8,2,32,128]{3,2,1,0:T(8,128)(2,1)}, f32[2,32,128]{2,1,0:T(8,128)}, f32[2,32,128]{2,1,0:T(8,128)}, f32[1,128]{1,0:T(1,128)}, f32[1,128]{1,0:T(1,128)}) custom-call(f32[64,2,128]{2,1,0:T(2,128)} %copy-done.3, f32[2,32,128]{2,1,0:T(8,128)} %get-tuple-element.17.gradient_ref, f32[2,32,128]{2,1,0:T(8,128)} %master_ref.1, ...), custom_call_target="tpu_custom_call" | custom-call | tf_op jit(solution)/shard_map/update/pallas_call | solution.py:158
  106.1 11.2 %all_to_all.32 = bf16[8,64,128]{2,1,0:T(8,128)(2,1)S(1)} all-to-all(bf16[8,64,128]{2,1,0:T(8,128)(2,1)} %bitcast.34), channel_id=1, replica_groups={{0,16,32,48,64,80,96,112},{128,144,160,176,192,208,224,240},{256,272,28..., dimensions={0} | all-to-all | bytes 262144 | tf_op jit(solution)/shard_map/all_to_all | solution.py:35
  117.3 0.1 broadcast_in_dim.19
  117.4 20.5 %all_to_all.33 = bf16[8,512,128]{2,1,0:T(8,128)(2,1)S(1)} all-to-all(bf16[8,512,128]{2,1,0:T(8,128)(2,1)S(1)} %broadcast_in_dim.19), channel_id=1, replica_groups={{0,128,256,384,512,640,768,896},{16,144,272,400,528,656,784,912},{32,16..., dimensions={0} | all-to-all | bytes 2097152 | tf_op jit(solution)/shard_map/all_to_all | solution.py:35
  137.9 0.0 copy-start
  137.9 5.8 %collective-permute-start.1 = (bf16[64,2,32,128]{3,2,1,0:T(8,128)(2,1)S(1)}, bf16[64,2,32,128]{3,2,1,0:T(8,128)(2,1)S(1)}, u32[]{:S(2)}, u32[]{:S(2)}) collective-permute-start(bf16[64,2,32,128]{3,2,1,0:T(8,128)(2,1)S(1)} %bitcast.26), channel_id=1, source_target_pairs={{0,8},{8,0},{1,9},{9,1},{2,10},{10,2},{3,11},{11,3},{4,12},{12,4},... | collective-permute-start | bytes 3145736 | tf_op jit(solution)/shard_map/ppermute | solution.py:39
  143.7 2.3 %collective-permute-done.1.got_ref = bf16[64,2,32,128]{3,2,1,0:T(8,128)(2,1)S(1)} collective-permute-done((bf16[64,2,32,128]{3,2,1,0:T(8,128)(2,1)S(1)}, bf16[64,2,32,128]{3,2,1,0:T(8,128)(2,1)S(1)}, u32[]{:S(2)}, u32[]{:S(2)}) %collective-permute-start.1) | collective-permute-done | bytes 1048608 | tf_op jit(solution)/shard_map/ppermute | solution.py:39
  145.9 0.0 copy-done
  146.0 0.0 copy-start.1
  146.0 1.0 copy-done.1
  147.0 3.5 %assemble.1 = bf16[2,64,2,32,128]{4,3,2,1,0:T(8,128)(2,1)} custom-call(s32[1]{0:T(128)} %bitcast.core_ref, bf16[64,2,32,128]{3,2,1,0:T(8,128)(2,1)} %bitcast.27, bf16[64,2,32,128]{3,2,1,0:T(8,128)(2,1)} %copy-done.1), custom_call_target="tpu_custom_call" | custom-call | tf_op jit(solution)/shard_map/assemble/pallas_call | solution.py:183
  (4 shorter events, 0.0 us)
Async XLA Ops:
  3.6 18.3 %collective-permute-start = (bf16[2,64,32,128]{3,2,1,0:T(8,128)(2,1)S(1)}, bf16[2,64,32,128]{3,2,1,0:T(8,128)(2,1)S(1)}, u32[]{:S(2)}, u32[]{:S(2)}) collective-permute-start(bf16[2,64,32,128]{3,2,1,0:T(8,128)(2,1)S(1)} %get-tuple-element.23), channel_id=1, source_target_pairs={{0,8},{8,0},{1,9},{9,1},{2,10},{10,2},{3,11},{11,3},{4,12},{12,4},... | collective-permute-start | bytes 3145736 | tf_op jit(solution)/shard_map/ppermute | solution.py:39
  21.9 1.0 copy-start.2
  26.6 1.9 %copy-start.5 = (f32[8,128]{1,0:T(8,128)S(1)}, f32[8,128]{1,0:T(8,128)}, u32[]{:S(2)}) copy-start(f32[8,128]{1,0:T(8,128)} %get-tuple-element.15) | copy-start | bytes 12292
  68.9 17.0 %all-to-all-start.2 = ((f32[16,2,128]{2,1,0:T(2,128)}), f32[16,2,128]{2,1,0:T(2,128)S(1)}, u32[]{:S(2)}, u32[]{:S(2)}) async-start(f32[16,2,128]{2,1,0:T(2,128)} %get-tuple-element.16), calls=%async_computation.2 | async-start | bytes 32768 | tf_op jit(solution)/shard_map/all_to_all | solution.py:35
  85.9 0.6 copy-start.4
  88.0 15.7 %all-to-all-start.3 = ((f32[64,2,128]{2,1,0:T(2,128)}), f32[64,2,128]{2,1,0:T(2,128)S(1)}, u32[]{:S(2)}, u32[]{:S(2)}) async-start(f32[64,2,128]{2,1,0:T(2,128)} %chip_stats.1), calls=%async_computation.3 | async-start | bytes 131072 | tf_op jit(solution)/shard_map/all_to_all | solution.py:35
  103.7 0.6 copy-start.3
  137.9 8.0 %copy-start = (bf16[8,512,128]{2,1,0:T(8,128)(2,1)}, bf16[8,512,128]{2,1,0:T(8,128)(2,1)S(1)}, u32[]{:S(2)}) copy-start(bf16[8,512,128]{2,1,0:T(8,128)(2,1)S(1)} %all_to_all.33) | copy-start | bytes 3145732
  137.9 8.0 %collective-permute-start.1 = (bf16[64,2,32,128]{3,2,1,0:T(8,128)(2,1)S(1)}, bf16[64,2,32,128]{3,2,1,0:T(8,128)(2,1)S(1)}, u32[]{:S(2)}, u32[]{:S(2)}) collective-permute-start(bf16[64,2,32,128]{3,2,1,0:T(8,128)(2,1)S(1)} %bitcast.26), channel_id=1, source_target_pairs={{0,8},{8,0},{1,9},{9,1},{2,10},{10,2},{3,11},{11,3},{4,12},{12,4},... | collective-permute-start | bytes 3145736 | tf_op jit(solution)/shard_map/ppermute | solution.py:39
  146.0 1.0 copy-start.1

commit v2 on v1

v2 whole, which is shorter than its diff:
```python
import jax
import jax.numpy as jnp
from jax import lax
from jax.experimental import pallas as pl
from jax.experimental.pallas import tpu as pltpu
from jax.sharding import Mesh
from jax.sharding import PartitionSpec as P

DIN = 4096
HEAD = 128
STEP = 2
DP = ("z", "y", "c")
NZ, NY, NC, NX = 8, 8, 2, 8
ROWS = 32
SECOND_FIX = 1.0 - 0.95**STEP
FIRST_FIX = 1.0 - 0.9**STEP
LOW = 2048.0
SMALL_VMEM = pltpu.CompilerParams(vmem_limit_bytes=12 * 1024 * 1024)
VMEM = pl.BlockSpec(memory_space=pltpu.VMEM)
SMEM = pl.BlockSpec(memory_space=pltpu.SMEM)


def flat(z, y, c):
    return (z * NY + y) * NC + c


FIRST = [[flat(z, y, 0) for z in range(NZ)] for y in range(NY)] + [
    [flat(z, y, 1) for y in range(NY)] for z in range(NZ)
]
SECOND = [[flat(z, y, 0) for y in range(NY)] for z in range(NZ)] + [
    [flat(z, y, 1) for z in range(NZ)] for y in range(NY)
]
STATS = [[device * NX + x for device in line for x in range(NX)] for line in FIRST]


def exchange(blocks, axes, groups):
    return lax.all_to_all(blocks, axes, split_axis=0, concat_axis=0, tiled=True, axis_index_groups=groups)


def swap_cores(x):
    return lax.ppermute(x, "c", [(0, 1), (1, 0)])


def power_of(values):
    return jnp.floor(jnp.log2(jnp.maximum(jnp.max(jnp.abs(values)), 2.0**-100)))


def as_half(values, power):
    return (values * jnp.exp2(14.0 - power)).astype(jnp.float16)


def in_two(values, power):
    scaled = values * jnp.exp2(14.0 - power)
    high = lax.reduce_precision(scaled, 5, 10)
    low = (scaled - high) * LOW
    return [high.astype(jnp.float16).reshape(2 * ROWS, HEAD), low.astype(jnp.float16).reshape(2 * ROWS, HEAD)]


def rows_of(*powers):
    lane = lax.broadcasted_iota(jnp.int32, (8, HEAD), 1)
    row = jnp.zeros((8, HEAD), jnp.float32)
    for k, power in enumerate(powers):
        row = jnp.where(lane == k, power, row)
    return row.astype(jnp.float16)


def out_of_two(high, low, scale):
    return (high.astype(jnp.float32) + low.astype(jnp.float32) * (1.0 / LOW)) * scale[:, None, None]


def scale_at(got, row, lane):
    return jnp.exp2(got[:, row, lane].astype(jnp.float32) - 14.0)


def core_stats_kernel(x_ref, got_ref, out_ref):
    everyone = jnp.sum(jnp.sum(got_ref[...], axis=0), axis=0)
    mine = jnp.sum(got_ref[:, x_ref[0]], axis=0)
    total = jnp.sum(everyone[0:1], axis=1, keepdims=True) + everyone[1:2]
    lane = lax.broadcasted_iota(jnp.int32, (1, HEAD), 1)
    out_ref[0:1] = mine[0:1]
    out_ref[1:2] = jnp.where(lane == 0, mine[1:2], total)


def core_stats(where, got):
    return pl.pallas_call(
        core_stats_kernel,
        in_specs=[SMEM, VMEM],
        out_specs=VMEM,
        out_shape=jax.ShapeDtypeStruct((2, HEAD), jnp.float32),
        compiler_params=SMALL_VMEM,
        name="core_stats",
    )(where, got)


def update_kernel(where_ref, stats_ref, other_ref, gradient_ref, master_ref, moment_ref, own_master_ref, own_moment_ref,
                  heads_ref, neurons_ref, params_ref, new_master_ref, new_moment_ref, new_heads_ref, new_neurons_ref):
    own = where_ref[1]
    stats = stats_ref[...] + other_ref[...]
    neuron_sq, other = stats[0:1], stats[1:2]
    lane = lax.broadcasted_iota(jnp.int32, (1, HEAD), 1)
    head_sq = jnp.broadcast_to(jnp.sum(jnp.where(lane == 0, other, 0.0), axis=1, keepdims=True), (1, HEAD))
    total = jnp.broadcast_to(jnp.sum(jnp.where(lane == 1, other, 0.0), axis=1, keepdims=True), (1, HEAD))
    clip = jnp.minimum(1.0, 256.0 / (jnp.sqrt(total) + 1e-06))
    new_heads = 0.95 * heads_ref[...] + 0.05 * clip * clip * head_sq / (DIN * HEAD)
    new_neurons = 0.95 * neurons_ref[...] + 0.05 * clip * clip * neuron_sq / DIN
    new_heads_ref[...] = new_heads
    new_neurons_ref[...] = new_neurons
    for p, second in ((0, new_heads), (1, new_neurons)):
        denom = jnp.sqrt(second / SECOND_FIX) + 1e-08

        def step(master, moment, gradient):
            new_moment = 0.9 * moment + 0.1 * clip * gradient
            update = new_moment / FIRST_FIX / denom
            return new_moment, master - 0.01 * (update + 0.1 * master)

        new_moment_ref[p], new_master_ref[p] = step(own_master_ref[p], own_moment_ref[p], gradient_ref[own, p])
        for k in range(8):
            _, new_master = step(master_ref[k, p], moment_ref[k, p], gradient_ref[k, p])
            params_ref[k, p] = new_master.astype(jnp.bfloat16)


def update_of(where, stats, other, gradient, master, moment, own_master, own_moment, heads, neurons):
    own = jax.ShapeDtypeStruct((2, ROWS, HEAD), jnp.float32)
    row = jax.ShapeDtypeStruct((1, HEAD), jnp.float32)
    return pl.pallas_call(
        update_kernel,
        in_specs=[SMEM] + [VMEM] * 9,
        out_specs=[VMEM] * 5,
        out_shape=[jax.ShapeDtypeStruct((8, 2, ROWS, HEAD), jnp.bfloat16), own, own, row, row],
        compiler_params=SMALL_VMEM,
        name="update",
    )(where, stats, other, gradient, master, moment, own_master, own_moment, heads, neurons)


def assemble_kernel(core_ref, mine_ref, got_ref, out_ref):
    core = core_ref[0]

    def place(i, carry):
        turned = (i % 8) * 8 + i // 8
        for p in range(2):
            out_ref[p, jnp.where(core == 0, i, turned), core] = mine_ref[i, p]
            out_ref[p, jnp.where(core == 0, turned, i), 1 - core] = got_ref[i, p]
        return carry

    lax.fori_loop(0, 64, place, 0, unroll=4)


def assemble(core, mine, got):
    return pl.pallas_call(
        assemble_kernel,
        in_specs=[SMEM, VMEM, VMEM],
        out_specs=VMEM,
        out_shape=jax.ShapeDtypeStruct((2, 64, 2, ROWS, HEAD), jnp.bfloat16),
        compiler_params=SMALL_VMEM,
        name="assemble",
    )(core, mine, got)


def on_device(grads, master, moment, v_heads, v_neurons):
    c = lax.axis_index("c")
    x = lax.axis_index("x")
    own = jnp.where(c == 0, lax.axis_index("y"), lax.axis_index("z"))

    where = jnp.stack([x, own]).astype(jnp.int32)
    core = c.reshape(1).astype(jnp.int32)
    halves = grads[0].reshape(2, 64, 2, ROWS, HEAD)
    theirs = lax.dynamic_index_in_dim(halves, 1 - c, 2, keepdims=False)
    halves, theirs = lax.optimization_barrier((halves, theirs))
    mine = lax.dynamic_index_in_dim(halves, c, 2, keepdims=False)
    power_a, power_o = power_of(master), power_of(moment)
    state = jnp.concatenate(in_two(master, power_a) + in_two(moment, power_o), axis=0)
    heads = jnp.broadcast_to(v_heads, (1, HEAD))
    neurons = v_neurons.reshape(1, HEAD)
    sums = mine.astype(jnp.float32) + swap_cores(theirs).astype(jnp.float32)
    power = power_of(sums)
    sums = sums.reshape(2, 8, 8, ROWS, HEAD)
    ordered = jnp.where(c == 0, sums.transpose(1, 2, 0, 3, 4), sums.transpose(2, 1, 0, 3, 4))
    message = jnp.concatenate(
        [as_half(ordered, power).reshape(8, 512, HEAD), jnp.broadcast_to(rows_of(power), (8, 8, HEAD))], axis=1
    )
    got = exchange(message, DP, FIRST)
    partial = jnp.sum(got[:, :512].astype(jnp.float32) * scale_at(got, 512, 0)[:, None, None], axis=0)

    power = power_of(partial)
    message = jnp.concatenate([as_half(partial, power), state, rows_of(power, power_a, power_o)], axis=0)
    message, where, core, heads = lax.optimization_barrier((message, where, core, heads))
    got = exchange(jnp.broadcast_to(message, (8, *message.shape)), DP, SECOND)
    gradient = jnp.sum(got[:, :512].astype(jnp.float32) * scale_at(got, 768, 0)[:, None, None], axis=0) / 128.0
    gradient = gradient.reshape(8, 2, ROWS, HEAD)
    squares = jnp.sum(gradient * gradient, axis=(0, 2))
    stats = jnp.stack([squares[1], jnp.broadcast_to(jnp.sum(squares[0]), (HEAD,))])
    stats = exchange(jnp.broadcast_to(stats, (64, 2, HEAD)), (*DP, "x"), STATS)
    stats = core_stats(where, stats.reshape(8, NX, 2, HEAD))

    line_master = out_of_two(got[:, 512:576], got[:, 576:640], scale_at(got, 768, 1)).reshape(8, 2, ROWS, HEAD)
    line_moment = out_of_two(got[:, 640:704], got[:, 704:768], scale_at(got, 768, 2)).reshape(8, 2, ROWS, HEAD)
    params, new_master, new_moment, new_heads, new_neurons = update_of(
        where, stats, swap_cores(stats), gradient, line_master, line_moment, master, moment, heads, neurons
    )
    plane = exchange(jnp.broadcast_to(params.reshape(512, HEAD), (8, 512, HEAD)), DP, FIRST)
    plane = plane.reshape(64, 2, ROWS, HEAD)
    params = assemble(core, plane, swap_cores(plane)).reshape(2, DIN, HEAD)
    return (params, new_master, new_moment, new_heads[0, :1], new_neurons.reshape(HEAD))


def solution(mesh):
    split = Mesh(mesh.devices.reshape(NZ, NY, NC, NX), ("z", "y", "c", "x"))
    return jax.shard_map(
        on_device,
        mesh=split,
        in_specs=(
            P(DP, None, None, "x"),
            P(None, DP, "x"),
            P(None, DP, "x"),
            P("x"),
            P("x"),
        ),
        out_specs=(
            P(None, None, "x"),
            P(None, DP, "x"),
            P(None, DP, "x"),
            P("x"),
            P("x"),
        ),
        check_vma=False,
    )
```

time: 151 us -> 139 us (0.921)
  blocking collectives: 69.7 us -> 50.8 us
  waiting for transfers between devices: 22 us -> 31 us
  Pallas kernels: 12.1 us -> 3.94 us
  other arithmetic: 2.46 us -> 7.37 us
  between operations: 1.37 us -> 4.48 us
  local copies, waits for them, and re-layouts: 6.44 us -> 3.83 us
    all_to_all x4 -> x2, blocking collectives: 69.7 us -> 50.8 us  [exchange(): lax.all_to_all(blocks, axes, split_axis=0, concat_axis=0, tiled=True, axi...]
    all_to_all x2, waiting for transfers between devices: 17.5 us -> 25.7 us  [exchange(): lax.all_to_all(blocks, axes, split_axis=0, concat_axis=0, tiled=True, axi...]
    pallas_call x5 -> x3, Pallas kernels: 12.1 us -> 3.94 us  [the longest x1 1.95 us: assemble(): pl.pallas_call(assemble_kernel, in_specs=[SMEM, VMEM, VMEM], out_specs=VM...]
    reduce_max x0 -> x4, other arithmetic: none -> 4 us  [power_of(): jnp.max(jnp.abs(values))]
    ppermute x2 -> x3, starting transfers between devices: 21.8 us -> 25.7 us  [swap_cores(): return lax.ppermute(x, 'c', [(0, 1), (1, 0)])]
    all_to_all x2, starting transfers between devices: 14.6 us -> 11.3 us  [exchange(): lax.all_to_all(blocks, axes, split_axis=0, concat_axis=0, tiled=True, axi...]
    unnamed x13 -> x14, local copies, waits for them, and re-layouts: 2.83 us -> 0.48 us
    squeeze x1, local copies, waits for them, and re-layouts: 2.95 us -> 1.32 us  [on_device(): theirs = lax.dynamic_index_in_dim(halves, 1 - c, 2, keepdims=False)]
  transfers between devices with their start and end apart: 4 -> 5, of which waited for: 4 -> 5; matrix products, arithmetic and copies ran while one was open for 0% -> 1% of each run, Pallas kernels for 0% -> 0%
where the time goes in v2:
time: 139 us; the launch traced here: 138 us
  blocking collectives  50.8 us (37%)
  starting transfers between devices  37 us (27%)
  waiting for transfers between devices  31 us (22%)
  other arithmetic  7.37 us (5%)
  between operations  4.48 us (3%)
  Pallas kernels  3.94 us (3%)
  local copies, waits for them, and re-layouts  3.83 us (3%)
    all_to_all x2, blocking collectives, exchange(): lax.all_to_all(blocks, axes, split_axis=0, concat_axis=0, tiled=True, axi...  50.8 us
    all_to_all x2, waiting for transfers between devices, exchange(): lax.all_to_all(blocks, axes, split_axis=0, concat_axis=0, tiled=True, axi...  25.7 us
    ppermute x3, starting transfers between devices, swap_cores(): return lax.ppermute(x, 'c', [(0, 1), (1, 0)])  25.7 us
    all_to_all x2, starting transfers between devices, exchange(): lax.all_to_all(blocks, axes, split_axis=0, concat_axis=0, tiled=True, axi...  11.3 us
    ppermute x3, waiting for transfers between devices, swap_cores(): return lax.ppermute(x, 'c', [(0, 1), (1, 0)])  5.21 us
    reduce_max x4, other arithmetic, power_of(): jnp.max(jnp.abs(values))  4 us
  transfers between devices with their start and end apart: 5, of which 5 were waited for; matrix products, arithmetic and copies ran while one was open for 1% of the time, Pallas kernels for 0%

profile of v2, /device:TPU:1, one launch (start us, length us, event | category | flops | bytes accessed | tf_op | source)
XLA Modules:
  0.0 138.4 jit_solution(16964787149843714410)
XLA Ops:
  0.6 1.3 dynamic-slice_bitcast_fusion
  2.0 16.0 %collective-permute-start = (bf16[2,64,32,128]{3,2,1,0:T(8,128)(2,1)S(1)}, bf16[2,64,32,128]{3,2,1,0:T(8,128)(2,1)S(1)}, u32[]{:S(2)}, u32[]{:S(2)}) collective-permute-start(bf16[2,64,32,128]{3,2,1,0:T(8,128)(2,1)S(1)} %dynamic-slice_bitcast_fusion), channel_id=1, source_target_pairs={{0,8},{8,0},{1,9},{9,1},{2,10},{10,2},{3,11},{11,3},{4,12},{12,4},... | collective-permute-start | bytes 3145736 | tf_op jit(solution)/shard_map/ppermute | solution.py:41
  18.0 2.3 %collective-permute-done = bf16[2,64,32,128]{3,2,1,0:T(8,128)(2,1)S(1)} collective-permute-done((bf16[2,64,32,128]{3,2,1,0:T(8,128)(2,1)S(1)}, bf16[2,64,32,128]{3,2,1,0:T(8,128)(2,1)S(1)}, u32[]{:S(2)}, u32[]{:S(2)}) %collective-permute-start) | collective-permute-done | bytes 1048608 | tf_op jit(solution)/shard_map/ppermute | solution.py:41
  20.3 2.2 %abs_reduce_fusion = (f32[]{:T(128)}, f32[2,64,32,128]{3,2,1,0:T(8,128)S(1)}) fusion(bf16[2,64,32,128]{3,2,1,0:T(8,128)(2,1)S(1)} %collective-permute-done, bf16[2,64,2,32,128]{4,3,2,1,0:T(8,128)(2,1)} %bitcast.58, s32[]{:T(128)S(6)} %select_n.36), kind=kLoop, calls=%fused_computation.6 | loop fusion | flops 2621439 | bytes 4194312 | tf_op jit(solution)/shard_map/reduce_max | solution.py:45
  23.2 0.5 fusion.1
  23.7 0.3 copy.19
  24.0 0.0 copy-start.1
  24.0 0.0 copy-start
  24.0 1.3 pad_maximum_fusion
  25.3 3.6 %all-to-all-start = ((f16[8,520,128]{2,1,0:T(8,128)(2,1)}), f16[8,520,128]{2,1,0:T(8,128)(2,1)S(1)}, u32[]{:S(2)}, u32[]{:S(2)}) async-start(f16[8,520,128]{2,1,0:T(8,128)(2,1)} %pad_maximum_fusion), calls=%async_computation | async-start | bytes 2129920 | tf_op jit(solution)/shard_map/all_to_all | solution.py:37
  29.5 0.0 copy-done.1
  29.5 0.6 abs_reduce_fusion.2
  30.9 0.0 copy-done
  30.9 0.6 abs_reduce_fusion.3
  32.2 0.1 pad_add_fusion.x_ref.where_ref
  32.4 14.7 %all-to-all-done = f16[8,520,128]{2,1,0:T(8,128)(2,1)S(1)} async-done(((f16[8,520,128]{2,1,0:T(8,128)(2,1)}), f16[8,520,128]{2,1,0:T(8,128)(2,1)S(1)}, u32[]{:S(2)}, u32[]{:S(2)}) %all-to-all-start) | async-done | bytes 1064992 | tf_op jit(solution)/shard_map/all_to_all | solution.py:37
  47.1 0.1 copy.24
  47.2 0.3 multiply_reduce_fusion.1
  47.5 0.6 abs_reduce_fusion.1
  49.0 0.2 broadcast_in_dim.40
  49.2 30.6 %all_to_all.20 = f16[8,776,128]{2,1,0:T(8,128)(2,1)S(1)} all-to-all(f16[8,776,128]{2,1,0:T(8,128)(2,1)S(1)} %broadcast_in_dim.40), channel_id=1, replica_groups={{0,16,32,48,64,80,96,112},{128,144,160,176,192,208,224,240},{256,272,28..., dimensions={0} | all-to-all | bytes 3178496 | tf_op jit(solution)/shard_map/all_to_all | solution.py:37
  79.8 0.0 copy-start.2
  79.8 0.1 fusion.8
  79.9 0.1 copy.27
  80.0 0.1 copy.26
  80.1 0.1 copy.25
  80.2 0.3 multiply_reduce_fusion
  80.6 0.1 multiply_reduce_fusion.2
  80.6 0.6 slice_reduce_fusion
  81.2 0.6 stack.15
  81.9 0.6 broadcast_in_dim.41
  82.5 7.7 %all-to-all-start.2 = ((f32[64,2,128]{2,1,0:T(2,128)}), f32[64,2,128]{2,1,0:T(2,128)S(1)}, u32[]{:S(2)}, u32[]{:S(2)}) async-start(f32[64,2,128]{2,1,0:T(2,128)} %broadcast_in_dim.41), calls=%async_computation.2 | async-start | bytes 131072 | tf_op jit(solution)/shard_map/all_to_all | solution.py:37
  90.3 11.1 %all-to-all-done.2 = f32[64,2,128]{2,1,0:T(2,128)S(1)} async-done(((f32[64,2,128]{2,1,0:T(2,128)}), f32[64,2,128]{2,1,0:T(2,128)S(1)}, u32[]{:S(2)}, u32[]{:S(2)}) %all-to-all-start.2) | async-done | bytes 65568 | tf_op jit(solution)/shard_map/all_to_all | solution.py:37
  101.4 0.6 core_stats.1.stats_ref
  102.0 6.3 %collective-permute-start.1 = (f32[2,128]{1,0:T(2,128)S(1)}, f32[2,128]{1,0:T(2,128)S(1)}, u32[]{:S(2)}, u32[]{:S(2)}) collective-permute-start(f32[2,128]{1,0:T(2,128)S(1)} %core_stats.1.stats_ref), channel_id=1, source_target_pairs={{0,8},{8,0},{1,9},{9,1},{2,10},{10,2},{3,11},{11,3},{4,12},{12,4},... | collective-permute-start | bytes 3080 | tf_op jit(solution)/shard_map/ppermute | solution.py:41
  108.3 0.1 add_multiply_fusion
  108.4 0.7 collective-permute-done.1.other_ref
  109.1 0.0 copy-done.2
  109.1 1.3 update.1
  110.5 0.1 broadcast_in_dim.42
  110.6 20.2 %all_to_all.21 = bf16[8,512,128]{2,1,0:T(8,128)(2,1)S(1)} all-to-all(bf16[8,512,128]{2,1,0:T(8,128)(2,1)S(1)} %broadcast_in_dim.42), channel_id=1, replica_groups={{0,128,256,384,512,640,768,896},{16,144,272,400,528,656,784,912},{32,16..., dimensions={0} | all-to-all | bytes 2097152 | tf_op jit(solution)/shard_map/all_to_all | solution.py:37
  130.8 3.4 %collective-permute-start.2 = (bf16[64,2,32,128]{3,2,1,0:T(8,128)(2,1)S(1)}, bf16[64,2,32,128]{3,2,1,0:T(8,128)(2,1)S(1)}, u32[]{:S(2)}, u32[]{:S(2)}) collective-permute-start(bf16[64,2,32,128]{3,2,1,0:T(8,128)(2,1)S(1)} %bitcast.45), channel_id=1, source_target_pairs={{0,8},{8,0},{1,9},{9,1},{2,10},{10,2},{3,11},{11,3},{4,12},{12,4},... | collective-permute-start | bytes 3145736 | tf_op jit(solution)/shard_map/ppermute | solution.py:41
  134.2 2.3 %collective-permute-done.2.got_ref = bf16[64,2,32,128]{3,2,1,0:T(8,128)(2,1)S(1)} collective-permute-done((bf16[64,2,32,128]{3,2,1,0:T(8,128)(2,1)S(1)}, bf16[64,2,32,128]{3,2,1,0:T(8,128)(2,1)S(1)}, u32[]{:S(2)}, u32[]{:S(2)}) %collective-permute-start.2) | collective-permute-done | bytes 1048608 | tf_op jit(solution)/shard_map/ppermute | solution.py:41
  136.4 2.0 %assemble.1 = bf16[2,64,2,32,128]{4,3,2,1,0:T(8,128)(2,1)} custom-call(s32[1]{0:T(128)} %bitcast.14.core_ref, bf16[64,2,32,128]{3,2,1,0:T(8,128)(2,1)S(1)} %bitcast.46, bf16[64,2,32,128]{3,2,1,0:T(8,128)(2,1)S(1)} %collective-permute-done.2.got_ref), custom_call_target="tpu_custom_call" | custom-call | tf_op jit(solution)/shard_map/assemble/pallas_call | solution.py:149
  (19 shorter events, 0.3 us)
Async XLA Ops:
  2.0 18.3 %collective-permute-start = (bf16[2,64,32,128]{3,2,1,0:T(8,128)(2,1)S(1)}, bf16[2,64,32,128]{3,2,1,0:T(8,128)(2,1)S(1)}, u32[]{:S(2)}, u32[]{:S(2)}) collective-permute-start(bf16[2,64,32,128]{3,2,1,0:T(8,128)(2,1)S(1)} %dynamic-slice_bitcast_fusion), channel_id=1, source_target_pairs={{0,8},{8,0},{1,9},{9,1},{2,10},{10,2},{3,11},{11,3},{4,12},{12,4},... | collective-permute-start | bytes 3145736 | tf_op jit(solution)/shard_map/ppermute | solution.py:41
  24.0 5.5 %copy-start.1 = (f32[2,32,128]{2,1,0:T(8,128)S(1)}, f32[2,32,128]{2,1,0:T(8,128)}, u32[]{:S(2)}) copy-start(f32[2,32,128]{2,1,0:T(8,128)} %own_moment_ref.1) | copy-start | bytes 98308
  24.0 6.8 %copy-start = (f32[2,32,128]{2,1,0:T(8,128)S(1)}, f32[2,32,128]{2,1,0:T(8,128)}, u32[]{:S(2)}) copy-start(f32[2,32,128]{2,1,0:T(8,128)} %own_master_ref.1) | copy-start | bytes 98308
  25.3 21.8 %all-to-all-start = ((f16[8,520,128]{2,1,0:T(8,128)(2,1)}), f16[8,520,128]{2,1,0:T(8,128)(2,1)S(1)}, u32[]{:S(2)}, u32[]{:S(2)}) async-start(f16[8,520,128]{2,1,0:T(8,128)(2,1)} %pad_maximum_fusion), calls=%async_computation | async-start | bytes 2129920 | tf_op jit(solution)/shard_map/all_to_all | solution.py:37
  79.8 29.3 %copy-start.2 = (f32[128]{0:T(128)S(1)}, f32[128]{0:T(128)}, u32[]{:S(2)}) copy-start(f32[128]{0:T(128)} %param.9) | copy-start | bytes 1540
  82.5 18.8 %all-to-all-start.2 = ((f32[64,2,128]{2,1,0:T(2,128)}), f32[64,2,128]{2,1,0:T(2,128)S(1)}, u32[]{:S(2)}, u32[]{:S(2)}) async-start(f32[64,2,128]{2,1,0:T(2,128)} %broadcast_in_dim.41), calls=%async_computation.2 | async-start | bytes 131072 | tf_op jit(solution)/shard_map/all_to_all | solution.py:37
  102.0 7.1 %collective-permute-start.1 = (f32[2,128]{1,0:T(2,128)S(1)}, f32[2,128]{1,0:T(2,128)S(1)}, u32[]{:S(2)}, u32[]{:S(2)}) collective-permute-start(f32[2,128]{1,0:T(2,128)S(1)} %core_stats.1.stats_ref), channel_id=1, source_target_pairs={{0,8},{8,0},{1,9},{9,1},{2,10},{10,2},{3,11},{11,3},{4,12},{12,4},... | collective-permute-start | bytes 3080 | tf_op jit(solution)/shard_map/ppermute | solution.py:41
  130.8 5.7 %collective-permute-start.2 = (bf16[64,2,32,128]{3,2,1,0:T(8,128)(2,1)S(1)}, bf16[64,2,32,128]{3,2,1,0:T(8,128)(2,1)S(1)}, u32[]{:S(2)}, u32[]{:S(2)}) collective-permute-start(bf16[64,2,32,128]{3,2,1,0:T(8,128)(2,1)S(1)} %bitcast.45), channel_id=1, source_target_pairs={{0,8},{8,0},{1,9},{9,1},{2,10},{10,2},{3,11},{11,3},{4,12},{12,4},... | collective-permute-start | bytes 3145736 | tf_op jit(solution)/shard_map/ppermute | solution.py:41

commit v3 on v2

--- a/solution.py
+++ b/solution.py
@@ -14,7 +14,6 @@
 ROWS = 32
 SECOND_FIX = 1.0 - 0.95**STEP
 FIRST_FIX = 1.0 - 0.9**STEP
-LOW = 2048.0
 SMALL_VMEM = pltpu.CompilerParams(vmem_limit_bytes=12 * 1024 * 1024)
 VMEM = pl.BlockSpec(memory_space=pltpu.VMEM)
 SMEM = pl.BlockSpec(memory_space=pltpu.SMEM)
@@ -49,27 +48,38 @@
     return (values * jnp.exp2(14.0 - power)).astype(jnp.float16)
 
 
-def in_two(values, power):
-    scaled = values * jnp.exp2(14.0 - power)
-    high = lax.reduce_precision(scaled, 5, 10)
-    low = (scaled - high) * LOW
-    return [high.astype(jnp.float16).reshape(2 * ROWS, HEAD), low.astype(jnp.float16).reshape(2 * ROWS, HEAD)]
-
-
-def rows_of(*powers):
-    lane = lax.broadcasted_iota(jnp.int32, (8, HEAD), 1)
-    row = jnp.zeros((8, HEAD), jnp.float32)
-    for k, power in enumerate(powers):
-        row = jnp.where(lane == k, power, row)
-    return row.astype(jnp.float16)
-
-
-def out_of_two(high, low, scale):
-    return (high.astype(jnp.float32) + low.astype(jnp.float32) * (1.0 / LOW)) * scale[:, None, None]
-
-
-def scale_at(got, row, lane):
-    return jnp.exp2(got[:, row, lane].astype(jnp.float32) - 14.0)
+def row_of(power):
+    return jnp.full((8, HEAD), power, jnp.float16)
+
+
+def scale_at(got):
+    return jnp.exp2(got[:, 512, 0].astype(jnp.float32) - 14.0)
+
+
+def summed(got):
+    return jnp.sum(got[:, :512].astype(jnp.float32) * scale_at(got)[:, None, None], axis=0)
+
+
+def line_stats_kernel(gradient_ref, out_ref):
+    squares = [jnp.zeros((1, HEAD), jnp.float32)] * 2
+    for p in range(2):
+        for k in range(8):
+            gradient = gradient_ref[k, p]
+            squares[p] = squares[p] + jnp.sum(gradient * gradient, axis=0, keepdims=True)
+    head = jnp.broadcast_to(jnp.sum(squares[0], axis=1, keepdims=True), (1, HEAD))
+    out_ref[:, 0:1] = jnp.broadcast_to(squares[1][None], (64, 1, HEAD))
+    out_ref[:, 1:2] = jnp.broadcast_to(head[None], (64, 1, HEAD))
+
+
+def line_stats(gradient):
+    return pl.pallas_call(
+        line_stats_kernel,
+        in_specs=[VMEM],
+        out_specs=VMEM,
+        out_shape=jax.ShapeDtypeStruct((64, 2, HEAD), jnp.float32),
+        compiler_params=SMALL_VMEM,
+        name="line_stats",
+    )(gradient)
 
 
 def core_stats_kernel(x_ref, got_ref, out_ref):
@@ -92,7 +102,7 @@
     )(where, got)
 
 
-def update_kernel(where_ref, stats_ref, other_ref, gradient_ref, master_ref, moment_ref, own_master_ref, own_moment_ref,
+def update_kernel(where_ref, stats_ref, other_ref, gradient_ref, state_ref,
                   heads_ref, neurons_ref, params_ref, new_master_ref, new_moment_ref, new_heads_ref, new_neurons_ref):
     own = where_ref[1]
     stats = stats_ref[...] + other_ref[...]
@@ -113,23 +123,23 @@
             update = new_moment / FIRST_FIX / denom
             return new_moment, master - 0.01 * (update + 0.1 * master)
 
-        new_moment_ref[p], new_master_ref[p] = step(own_master_ref[p], own_moment_ref[p], gradient_ref[own, p])
+        new_moment_ref[p], new_master_ref[p] = step(state_ref[own, 0, p], state_ref[own, 1, p], gradient_ref[own, p])
         for k in range(8):
-            _, new_master = step(master_ref[k, p], moment_ref[k, p], gradient_ref[k, p])
+            _, new_master = step(state_ref[k, 0, p], state_ref[k, 1, p], gradient_ref[k, p])
             params_ref[k, p] = new_master.astype(jnp.bfloat16)
 
 
-def update_of(where, stats, other, gradient, master, moment, own_master, own_moment, heads, neurons):
+def update_of(where, stats, other, gradient, state, heads, neurons):
     own = jax.ShapeDtypeStruct((2, ROWS, HEAD), jnp.float32)
     row = jax.ShapeDtypeStruct((1, HEAD), jnp.float32)
     return pl.pallas_call(
         update_kernel,
-        in_specs=[SMEM] + [VMEM] * 9,
+        in_specs=[SMEM] + [VMEM] * 6,
         out_specs=[VMEM] * 5,
         out_shape=[jax.ShapeDtypeStruct((8, 2, ROWS, HEAD), jnp.bfloat16), own, own, row, row],
         compiler_params=SMALL_VMEM,
         name="update",
-    )(where, stats, other, gradient, master, moment, own_master, own_moment, heads, neurons)
+    )(where, stats, other, gradient, state, heads, neurons)
 
 
 def assemble_kernel(core_ref, mine_ref, got_ref, out_ref):
@@ -163,12 +173,12 @@
 
     where = jnp.stack([x, own]).astype(jnp.int32)
     core = c.reshape(1).astype(jnp.int32)
+    state = jnp.broadcast_to(jnp.stack([master, moment]).reshape(4 * ROWS, HEAD), (8, 4 * ROWS, HEAD))
+    state = exchange(state, DP, SECOND)
     halves = grads[0].reshape(2, 64, 2, ROWS, HEAD)
     theirs = lax.dynamic_index_in_dim(halves, 1 - c, 2, keepdims=False)
     halves, theirs = lax.optimization_barrier((halves, theirs))
     mine = lax.dynamic_index_in_dim(halves, c, 2, keepdims=False)
-    power_a, power_o = power_of(master), power_of(moment)
-    state = jnp.concatenate(in_two(master, power_a) + in_two(moment, power_o), axis=0)
     heads = jnp.broadcast_to(v_heads, (1, HEAD))
     neurons = v_neurons.reshape(1, HEAD)
     sums = mine.astype(jnp.float32) + swap_cores(theirs).astype(jnp.float32)
@@ -176,26 +186,21 @@
     sums = sums.reshape(2, 8, 8, ROWS, HEAD)
     ordered = jnp.where(c == 0, sums.transpose(1, 2, 0, 3, 4), sums.transpose(2, 1, 0, 3, 4))
     message = jnp.concatenate(
-        [as_half(ordered, power).reshape(8, 512, HEAD), jnp.broadcast_to(rows_of(power), (8, 8, HEAD))], axis=1
+        [as_half(ordered, power).reshape(8, 512, HEAD), jnp.broadcast_to(row_of(power), (8, 8, HEAD))], axis=1
     )
-    got = exchange(message, DP, FIRST)
-    partial = jnp.sum(got[:, :512].astype(jnp.float32) * scale_at(got, 512, 0)[:, None, None], axis=0)
+    message, where, core, heads, state = lax.optimization_barrier((message, where, core, heads, state))
+    partial = summed(exchange(message, DP, FIRST))
 
     power = power_of(partial)
-    message = jnp.concatenate([as_half(partial, power), state, rows_of(power, power_a, power_o)], axis=0)
-    message, where, core, heads = lax.optimization_barrier((message, where, core, heads))
+    message = lax.optimization_barrier(jnp.concatenate([as_half(partial, power), row_of(power)], axis=0))
     got = exchange(jnp.broadcast_to(message, (8, *message.shape)), DP, SECOND)
-    gradient = jnp.sum(got[:, :512].astype(jnp.float32) * scale_at(got, 768, 0)[:, None, None], axis=0) / 128.0
-    gradient = gradient.reshape(8, 2, ROWS, HEAD)
-    squares = jnp.sum(gradient * gradient, axis=(0, 2))
-    stats = jnp.stack([squares[1], jnp.broadcast_to(jnp.sum(squares[0]), (HEAD,))])
-    stats = exchange(jnp.broadcast_to(stats, (64, 2, HEAD)), (*DP, "x"), STATS)
+    gradient = (summed(got) / 128.0).reshape(8, 2, ROWS, HEAD)
+
+    stats = line_stats(gradient)
+    stats = exchange(stats, (*DP, "x"), STATS)
     stats = core_stats(where, stats.reshape(8, NX, 2, HEAD))
-
-    line_master = out_of_two(got[:, 512:576], got[:, 576:640], scale_at(got, 768, 1)).reshape(8, 2, ROWS, HEAD)
-    line_moment = out_of_two(got[:, 640:704], got[:, 704:768], scale_at(got, 768, 2)).reshape(8, 2, ROWS, HEAD)
     params, new_master, new_moment, new_heads, new_neurons = update_of(
-        where, stats, swap_cores(stats), gradient, line_master, line_moment, master, moment, heads, neurons
+        where, stats, swap_cores(stats), gradient, state.reshape(8, 2, 2, ROWS, HEAD), heads, neurons
     )
     plane = exchange(jnp.broadcast_to(params.reshape(512, HEAD), (8, 512, HEAD)), DP, FIRST)
     plane = plane.reshape(64, 2, ROWS, HEAD)

time: 139 us -> 140 us (level)
  blocking collectives: 50.8 us -> 84.2 us
  waiting for transfers between devices: 31 us -> 10.5 us
  starting transfers between devices: 37 us -> 29.9 us
  other arithmetic: 7.37 us -> 4.38 us
  between operations: 4.48 us -> 2.94 us
    all_to_all x2 -> x4, blocking collectives: 50.8 us -> 84.2 us  [exchange(): lax.all_to_all(blocks, axes, split_axis=0, concat_axis=0, tiled=True, axi...]
    all_to_all x2 -> x1, waiting for transfers between devices: 25.7 us -> 7.42 us  [exchange(): lax.all_to_all(blocks, axes, split_axis=0, concat_axis=0, tiled=True, axi...]
    all_to_all x2 -> x1, starting transfers between devices: 11.3 us -> 3.78 us  [exchange(): lax.all_to_all(blocks, axes, split_axis=0, concat_axis=0, tiled=True, axi...]
    ppermute x3, waiting for transfers between devices: 5.21 us -> 3.06 us  [swap_cores(): return lax.ppermute(x, 'c', [(0, 1), (1, 0)])]
    reduce_max x4 -> x2, other arithmetic: 4 us -> 3.13 us  [power_of(): jnp.max(jnp.abs(values))]
  transfers between devices with their start and end apart: 5 -> 4, of which waited for: 5 -> 3; matrix products, arithmetic and copies ran while one was open for 1% -> 3% of each run, Pallas kernels for 0% -> 0%
where the time goes in v3:
time: 140 us; the launch traced here: 139 us
  blocking collectives  84.2 us (60%)
  starting transfers between devices  29.9 us (21%)
  waiting for transfers between devices  10.5 us (8%)
  other arithmetic  4.38 us (3%)
  Pallas kernels  4.05 us (3%)
  local copies, waits for them, and re-layouts  3.2 us (2%)
  between operations  2.94 us (2%)
    all_to_all x4, blocking collectives, exchange(): lax.all_to_all(blocks, axes, split_axis=0, concat_axis=0, tiled=True, axi...  84.2 us
    ppermute x3, starting transfers between devices, swap_cores(): return lax.ppermute(x, 'c', [(0, 1), (1, 0)])  26.2 us
    all_to_all x1, waiting for transfers between devices, exchange(): lax.all_to_all(blocks, axes, split_axis=0, concat_axis=0, tiled=True, axi...  7.42 us
    all_to_all x1, starting transfers between devices, exchange(): lax.all_to_all(blocks, axes, split_axis=0, concat_axis=0, tiled=True, axi...  3.78 us
    reduce_max x2, other arithmetic, power_of(): jnp.max(jnp.abs(values))  3.13 us
    ppermute x3, waiting for transfers between devices, swap_cores(): return lax.ppermute(x, 'c', [(0, 1), (1, 0)])  3.06 us
  transfers between devices with their start and end apart: 4, of which 3 were waited for; matrix products, arithmetic and copies ran while one was open for 3% of the time, Pallas kernels for 0%

profile of v3, /device:TPU:1, one launch (start us, length us, event | category | flops | bytes accessed | tf_op | source)
XLA Modules:
  0.0 139.2 jit_solution(1443170188712432293)
XLA Ops:
  0.6 0.0 copy-start.1
  0.6 0.0 copy-start.2
  0.7 1.3 dynamic-slice_bitcast_fusion
  2.0 16.0 %collective-permute-start = (bf16[2,64,32,128]{3,2,1,0:T(8,128)(2,1)S(1)}, bf16[2,64,32,128]{3,2,1,0:T(8,128)(2,1)}, u32[]{:S(2)}, u32[]{:S(2)}) collective-permute-start(bf16[2,64,32,128]{3,2,1,0:T(8,128)(2,1)S(1)} %dynamic-slice_bitcast_fusion), channel_id=1, source_target_pairs={{0,8},{8,0},{1,9},{9,1},{2,10},{10,2},{3,11},{11,3},{4,12},{12,4},... | collective-permute-start | bytes 3145736 | tf_op jit(solution)/shard_map/ppermute | solution.py:40
  18.0 0.0 copy-done.1
  18.0 0.0 copy-done.2
  18.0 0.8 broadcast_in_dim.18
  18.9 3.8 %all-to-all-start = ((f32[8,128,128]{2,1,0:T(8,128)}), f32[8,128,128]{2,1,0:T(8,128)S(1)}, u32[]{:S(2)}, u32[]{:S(2)}) async-start(f32[8,128,128]{2,1,0:T(8,128)} %broadcast_in_dim.18), calls=%async_computation | async-start | bytes 1048576 | tf_op jit(solution)/shard_map/all_to_all | solution.py:36
  23.3 0.1 pad_add_fusion.x_ref.where_ref
  23.4 0.0 collective-permute-done
  23.4 2.5 %abs_reduce_fusion = (f32[]{:T(128)}, f32[2,64,32,128]{3,2,1,0:T(8,128)S(1)}) fusion(bf16[2,64,32,128]{3,2,1,0:T(8,128)(2,1)} %collective-permute-done, bf16[2,64,2,32,128]{4,3,2,1,0:T(8,128)(2,1)} %bitcast.51, s32[]{:T(128)S(6)} %select_n.21), kind=kLoop, calls=%fused_computation.6 | loop fusion | flops 2621439 | bytes 4194312 | tf_op jit(solution)/shard_map/reduce_max | solution.py:44
  26.6 0.5 fusion.1
  27.2 0.3 copy.17
  27.5 0.2 concatenate.6
  27.7 7.4 %all-to-all-done = f32[8,128,128]{2,1,0:T(8,128)S(1)} async-done(((f32[8,128,128]{2,1,0:T(8,128)}), f32[8,128,128]{2,1,0:T(8,128)S(1)}, u32[]{:S(2)}, u32[]{:S(2)}) %all-to-all-start) | async-done | bytes 524320 | tf_op jit(solution)/shard_map/all_to_all | solution.py:36
  35.1 24.7 %all_to_all.25 = f16[8,520,128]{2,1,0:T(8,128)(2,1)S(1)} all-to-all(f16[8,520,128]{2,1,0:T(8,128)(2,1)S(1)} %concatenate.6), channel_id=1, replica_groups={{0,128,256,384,512,640,768,896},{16,144,272,400,528,656,784,912},{32,16..., dimensions={0} | all-to-all | bytes 2129920 | tf_op jit(solution)/shard_map/all_to_all | solution.py:36
  59.8 0.1 copy.20
  59.9 0.3 multiply_reduce_fusion.1
  60.2 0.6 abs_reduce_fusion.1
  61.7 0.1 broadcast_in_dim.19
  61.8 0.0 copy-start
  61.8 20.6 %all_to_all.26 = f16[8,520,128]{2,1,0:T(8,128)(2,1)S(1)} all-to-all(f16[8,520,128]{2,1,0:T(8,128)(2,1)S(1)} %broadcast_in_dim.19), channel_id=1, replica_groups={{0,16,32,48,64,80,96,112},{128,144,160,176,192,208,224,240},{256,272,28..., dimensions={0} | all-to-all | bytes 2129920 | tf_op jit(solution)/shard_map/all_to_all | solution.py:36
  82.5 0.1 copy.21
  82.6 0.3 multiply_reduce_fusion
  82.9 0.1 line_stats.1
  83.0 18.7 %all_to_all.27 = f32[64,2,128]{2,1,0:T(2,128)S(1)} all-to-all(f32[64,2,128]{2,1,0:T(2,128)S(1)} %line_stats.1), channel_id=1, replica_groups={{0,1,2,3,4,5,6,7,128,129,130,131,132,133,134,135,256,257,258,259,260,26..., dimensions={0} | all-to-all | bytes 131072 | tf_op jit(solution)/shard_map/all_to_all | solution.py:36
  101.7 0.6 core_stats.1.stats_ref
  102.4 6.8 %collective-permute-start.1 = (f32[2,128]{1,0:T(2,128)S(1)}, f32[2,128]{1,0:T(2,128)S(1)}, u32[]{:S(2)}, u32[]{:S(2)}) collective-permute-start(f32[2,128]{1,0:T(2,128)S(1)} %core_stats.1.stats_ref), channel_id=1, source_target_pairs={{0,8},{8,0},{1,9},{9,1},{2,10},{10,2},{3,11},{11,3},{4,12},{12,4},... | collective-permute-start | bytes 3080 | tf_op jit(solution)/shard_map/ppermute | solution.py:40
  109.1 0.8 collective-permute-done.1.other_ref
  109.9 0.0 copy-done
  109.9 1.3 update.1
  111.3 0.1 broadcast_in_dim.20
  111.4 20.2 %all_to_all.28 = bf16[8,512,128]{2,1,0:T(8,128)(2,1)S(1)} all-to-all(bf16[8,512,128]{2,1,0:T(8,128)(2,1)S(1)} %broadcast_in_dim.20), channel_id=1, replica_groups={{0,128,256,384,512,640,768,896},{16,144,272,400,528,656,784,912},{32,16..., dimensions={0} | all-to-all | bytes 2097152 | tf_op jit(solution)/shard_map/all_to_all | solution.py:36
  131.6 3.4 %collective-permute-start.2 = (bf16[64,2,32,128]{3,2,1,0:T(8,128)(2,1)S(1)}, bf16[64,2,32,128]{3,2,1,0:T(8,128)(2,1)S(1)}, u32[]{:S(2)}, u32[]{:S(2)}) collective-permute-start(bf16[64,2,32,128]{3,2,1,0:T(8,128)(2,1)S(1)} %bitcast.39), channel_id=1, source_target_pairs={{0,8},{8,0},{1,9},{9,1},{2,10},{10,2},{3,11},{11,3},{4,12},{12,4},... | collective-permute-start | bytes 3145736 | tf_op jit(solution)/shard_map/ppermute | solution.py:40
  135.0 2.3 %collective-permute-done.2.got_ref = bf16[64,2,32,128]{3,2,1,0:T(8,128)(2,1)S(1)} collective-permute-done((bf16[64,2,32,128]{3,2,1,0:T(8,128)(2,1)S(1)}, bf16[64,2,32,128]{3,2,1,0:T(8,128)(2,1)S(1)}, u32[]{:S(2)}, u32[]{:S(2)}) %collective-permute-start.2) | collective-permute-done | bytes 1048608 | tf_op jit(solution)/shard_map/ppermute | solution.py:40
  137.2 2.0 %assemble.1 = bf16[2,64,2,32,128]{4,3,2,1,0:T(8,128)(2,1)} custom-call(s32[1]{0:T(128)} %bitcast.9.core_ref, bf16[64,2,32,128]{3,2,1,0:T(8,128)(2,1)S(1)} %bitcast.40, bf16[64,2,32,128]{3,2,1,0:T(8,128)(2,1)S(1)} %collective-permute-done.2.got_ref), custom_call_target="tpu_custom_call" | custom-call | tf_op jit(solution)/shard_map/assemble/pallas_call | solution.py:159
  (9 shorter events, 0.1 us)
Async XLA Ops:
  0.6 17.4 %copy-start.1 = (f32[2,32,128]{2,1,0:T(8,128)S(1)}, f32[2,32,128]{2,1,0:T(8,128)}, u32[]{:S(2)}) copy-start(f32[2,32,128]{2,1,0:T(8,128)} %param.7) | copy-start | bytes 98308
  0.6 17.4 %copy-start.2 = (f32[2,32,128]{2,1,0:T(8,128)S(1)}, f32[2,32,128]{2,1,0:T(8,128)}, u32[]{:S(2)}) copy-start(f32[2,32,128]{2,1,0:T(8,128)} %param.6) | copy-start | bytes 98308
  2.0 21.4 %collective-permute-start = (bf16[2,64,32,128]{3,2,1,0:T(8,128)(2,1)S(1)}, bf16[2,64,32,128]{3,2,1,0:T(8,128)(2,1)}, u32[]{:S(2)}, u32[]{:S(2)}) collective-permute-start(bf16[2,64,32,128]{3,2,1,0:T(8,128)(2,1)S(1)} %dynamic-slice_bitcast_fusion), channel_id=1, source_target_pairs={{0,8},{8,0},{1,9},{9,1},{2,10},{10,2},{3,11},{11,3},{4,12},{12,4},... | collective-permute-start | bytes 3145736 | tf_op jit(solution)/shard_map/ppermute | solution.py:40
  18.9 16.2 %all-to-all-start = ((f32[8,128,128]{2,1,0:T(8,128)}), f32[8,128,128]{2,1,0:T(8,128)S(1)}, u32[]{:S(2)}, u32[]{:S(2)}) async-start(f32[8,128,128]{2,1,0:T(8,128)} %broadcast_in_dim.18), calls=%async_computation | async-start | bytes 1048576 | tf_op jit(solution)/shard_map/all_to_all | solution.py:36
  61.8 48.1 %copy-start = (f32[128]{0:T(128)S(1)}, f32[128]{0:T(128)}, u32[]{:S(2)}) copy-start(f32[128]{0:T(128)} %param.9) | copy-start | bytes 1540
  102.4 7.6 %collective-permute-start.1 = (f32[2,128]{1,0:T(2,128)S(1)}, f32[2,128]{1,0:T(2,128)S(1)}, u32[]{:S(2)}, u32[]{:S(2)}) collective-permute-start(f32[2,128]{1,0:T(2,128)S(1)} %core_stats.1.stats_ref), channel_id=1, source_target_pairs={{0,8},{8,0},{1,9},{9,1},{2,10},{10,2},{3,11},{11,3},{4,12},{12,4},... | collective-permute-start | bytes 3080 | tf_op jit(solution)/shard_map/ppermute | solution.py:40
  131.6 5.7 %collective-permute-start.2 = (bf16[64,2,32,128]{3,2,1,0:T(8,128)(2,1)S(1)}, bf16[64,2,32,128]{3,2,1,0:T(8,128)(2,1)S(1)}, u32[]{:S(2)}, u32[]{:S(2)}) collective-permute-start(bf16[64,2,32,128]{3,2,1,0:T(8,128)(2,1)S(1)} %bitcast.39), channel_id=1, source_target_pairs={{0,8},{8,0},{1,9},{9,1},{2,10},{10,2},{3,11},{11,3},{4,12},{12,4},... | collective-permute-start | bytes 3145736 | tf_op jit(solution)/shard_map/ppermute | solution.py:40

commit v4 on v2

v4 whole, which is shorter than its diff:
```python
import jax
import jax.numpy as jnp
from jax import lax
from jax.experimental import pallas as pl
from jax.experimental.pallas import tpu as pltpu
from jax.sharding import Mesh
from jax.sharding import PartitionSpec as P

DIN = 4096
HEAD = 128
STEP = 2
DP = ("z", "y", "c")
NZ, NY, NC, NX = 8, 8, 2, 8
ROWS = 32
SECOND_FIX = 1.0 - 0.95**STEP
FIRST_FIX = 1.0 - 0.9**STEP
LOW = 2048.0
SMALL_VMEM = pltpu.CompilerParams(vmem_limit_bytes=12 * 1024 * 1024)
VMEM = pl.BlockSpec(memory_space=pltpu.VMEM)
SMEM = pl.BlockSpec(memory_space=pltpu.SMEM)
HBM = pl.BlockSpec(memory_space=pltpu.HBM)


def flat(z, y, c):
    return (z * NY + y) * NC + c


FIRST = [[flat(z, y, 0) for z in range(NZ)] for y in range(NY)] + [
    [flat(z, y, 1) for y in range(NY)] for z in range(NZ)
]
SECOND = [[flat(z, y, 0) for y in range(NY)] for z in range(NZ)] + [
    [flat(z, y, 1) for z in range(NZ)] for y in range(NY)
]
STATS = [
    [flat(z, j, 0) * NX + x for z in range(NZ) for x in range(NX)]
    + [flat(j, y, 1) * NX + x for y in range(NY) for x in range(NX)]
    for j in range(8)
]


def exchange(blocks, axes, groups):
    return lax.all_to_all(blocks, axes, split_axis=0, concat_axis=0, tiled=True, axis_index_groups=groups)


def swap_cores(x):
    return lax.ppermute(x, "c", [(0, 1), (1, 0)])


def power_of(values):
    return jnp.floor(jnp.log2(jnp.maximum(jnp.max(jnp.abs(values)), 2.0**-100)))


def as_half(values, power):
    return (values * jnp.exp2(14.0 - power)).astype(jnp.float16)


def in_two(values, power):
    scaled = values * jnp.exp2(14.0 - power)
    high = lax.reduce_precision(scaled, 5, 10)
    low = (scaled - high) * LOW
    return [high.astype(jnp.float16).reshape(2 * ROWS, HEAD), low.astype(jnp.float16).reshape(2 * ROWS, HEAD)]


def lane_row(k, power):
    lane = lax.broadcasted_iota(jnp.int32, (8, HEAD), 1)
    return jnp.where(lane == k, power, 0.0)


def out_of_two(high, low, scale):
    return (high.astype(jnp.float32) + low.astype(jnp.float32) * (1.0 / LOW)) * scale[:, None, None]


def scale_at(got, row, lane):
    return jnp.exp2(got[:, row, lane].astype(jnp.float32) - 14.0)


def line_stats_kernel(gradient_ref, out_ref):
    squares = [jnp.zeros((1, HEAD), jnp.float32)] * 2
    for p in range(2):
        for k in range(8):
            gradient = gradient_ref[k, p]
            squares[p] = squares[p] + jnp.sum(gradient * gradient, axis=0, keepdims=True)
    head = jnp.broadcast_to(jnp.sum(squares[0], axis=1, keepdims=True), (1, HEAD))
    out_ref[:, 0:1] = jnp.broadcast_to(squares[1][None], (128, 1, HEAD))
    out_ref[:, 1:2] = jnp.broadcast_to(head[None], (128, 1, HEAD))


def line_stats(gradient):
    return pl.pallas_call(
        line_stats_kernel,
        in_specs=[VMEM],
        out_specs=VMEM,
        out_shape=jax.ShapeDtypeStruct((128, 2, HEAD), jnp.float32),
        compiler_params=SMALL_VMEM,
        name="line_stats",
    )(gradient)


def update_kernel(where_ref, stats_ref, gradient_ref, master_ref, moment_ref, own_master_ref, own_moment_ref,
                  heads_ref, neurons_ref, params_ref, new_master_ref, new_moment_ref, new_heads_ref, new_neurons_ref):
    x, own = where_ref[0], where_ref[1]
    column = jnp.sum(jnp.sum(stats_ref[...], axis=0), axis=0)
    total = jnp.sum(column[0:1], axis=1, keepdims=True) + column[1:2]
    mine = jnp.sum(stats_ref[:, x], axis=0)
    neuron_sq, head_sq = mine[0:1], mine[1:2]
    clip = jnp.minimum(1.0, 256.0 / (jnp.sqrt(total) + 1e-06))
    new_heads = 0.95 * heads_ref[...] + 0.05 * clip * clip * head_sq / (DIN * HEAD)
    new_neurons = 0.95 * neurons_ref[...] + 0.05 * clip * clip * neuron_sq / DIN
    new_heads_ref[...] = new_heads
    new_neurons_ref[...] = new_neurons
    for p, second in ((0, new_heads), (1, new_neurons)):
        denom = jnp.sqrt(second / SECOND_FIX) + 1e-08

        def step(master, moment, gradient):
            new_moment = 0.9 * moment + 0.1 * clip * gradient
            update = new_moment / FIRST_FIX / denom
            return new_moment, master - 0.01 * (update + 0.1 * master)

        new_moment_ref[p], new_master_ref[p] = step(own_master_ref[p], own_moment_ref[p], gradient_ref[own, p])
        for k in range(8):
            _, new_master = step(master_ref[k, p], moment_ref[k, p], gradient_ref[k, p])
            params_ref[k, p] = new_master.astype(jnp.bfloat16)


def update_of(where, stats, gradient, master, moment, own_master, own_moment, heads, neurons):
    own = jax.ShapeDtypeStruct((2, ROWS, HEAD), jnp.float32)
    row = jax.ShapeDtypeStruct((1, HEAD), jnp.float32)
    return pl.pallas_call(
        update_kernel,
        in_specs=[SMEM] + [VMEM] * 8,
        out_specs=[VMEM] * 5,
        out_shape=[jax.ShapeDtypeStruct((8, 2, ROWS, HEAD), jnp.bfloat16), own, own, row, row],
        compiler_params=SMALL_VMEM,
        name="update",
    )(where, stats, gradient, master, moment, own_master, own_moment, heads, neurons)


def place_kernel(slot_ref, plane_ref, *rest):
    out_ref, sems = rest[-2:]
    slot = slot_ref[0]

    def copies(k):
        for hi in range(8):
            for p in range(2):
                source = plane_ref.at[hi, :, p] if k == 0 else plane_ref.at[:, hi, p]
                yield pltpu.make_async_copy(source, out_ref.at[p, hi, :, k], sems.at[hi, p])

    for k in range(2):

        @pl.when(slot == k)
        def _():
            for copy in copies(k):
                copy.start()
            for copy in copies(k):
                copy.wait()


def place(slot, plane, before, name):
    before = () if before is None else (before,)
    return pl.pallas_call(
        place_kernel,
        in_specs=[SMEM, VMEM] + [HBM] * len(before),
        out_specs=HBM,
        out_shape=jax.ShapeDtypeStruct((2, 8, 8, 2, ROWS, HEAD), jnp.bfloat16),
        scratch_shapes=[pltpu.SemaphoreType.DMA((8, 2))],
        input_output_aliases={2: 0} if before else {},
        compiler_params=SMALL_VMEM,
        name=name,
    )(slot, plane, *before)


def on_device(grads, master, moment, v_heads, v_neurons):
    c = lax.axis_index("c")
    x = lax.axis_index("x")
    own = jnp.where(c == 0, lax.axis_index("y"), lax.axis_index("z"))

    where = jnp.stack([x, own]).astype(jnp.int32)
    core = c.reshape(1).astype(jnp.int32)
    halves = grads[0].reshape(2, 64, 2, ROWS, HEAD)
    theirs = lax.dynamic_index_in_dim(halves, 1 - c, 2, keepdims=False)
    halves, theirs = lax.optimization_barrier((halves, theirs))
    mine = lax.dynamic_index_in_dim(halves, c, 2, keepdims=False)
    power_a, power_o = power_of(master), power_of(moment)
    state = jnp.concatenate(in_two(master, power_a) + in_two(moment, power_o), axis=0)
    heads = jnp.broadcast_to(v_heads, (1, HEAD))
    neurons = v_neurons.reshape(1, HEAD)
    sums = mine.astype(jnp.float32) + swap_cores(theirs).astype(jnp.float32)
    power = power_of(sums)
    sums = sums.reshape(2, 8, 8, ROWS, HEAD)
    ordered = jnp.where(c == 0, sums.transpose(1, 2, 0, 3, 4), sums.transpose(2, 1, 0, 3, 4))
    message = jnp.concatenate(
        [as_half(ordered, power).reshape(8, 512, HEAD), jnp.broadcast_to(lane_row(0, power).astype(jnp.float16), (8, 8, HEAD))], axis=1
    )
    first_lane, powers = lane_row(0, 1.0), lane_row(1, power_a) + lane_row(2, power_o)
    message, state, first_lane, powers, where, core, heads = lax.optimization_barrier(
        (message, state, first_lane, powers, where, core, heads)
    )
    got = exchange(message, DP, FIRST)
    partial = jnp.sum(got[:, :512].astype(jnp.float32) * scale_at(got, 512, 0)[:, None, None], axis=0)

    power = power_of(partial)
    message = jnp.concatenate([as_half(partial, power), state, (powers + power * first_lane).astype(jnp.float16)], axis=0)
    message = lax.optimization_barrier(message)
    got = exchange(jnp.broadcast_to(message, (8, *message.shape)), DP, SECOND)
    gradient = jnp.sum(got[:, :512].astype(jnp.float32) * scale_at(got, 768, 0)[:, None, None], axis=0) / 128.0
    gradient = gradient.reshape(8, 2, ROWS, HEAD)
    stats = exchange(line_stats(gradient), (*DP, "x"), STATS)
    line_master = out_of_two(got[:, 512:576], got[:, 576:640], scale_at(got, 768, 1)).reshape(8, 2, ROWS, HEAD)
    line_moment = out_of_two(got[:, 640:704], got[:, 704:768], scale_at(got, 768, 2)).reshape(8, 2, ROWS, HEAD)
    params, new_master, new_moment, new_heads, new_neurons = update_of(
        where, stats.reshape(16, NX, 2, HEAD), gradient, line_master, line_moment, master, moment, heads, neurons
    )
    plane = exchange(jnp.broadcast_to(params.reshape(512, HEAD), (8, 512, HEAD)), DP, FIRST)
    plane = plane.reshape(8, 8, 2, ROWS, HEAD)
    other = swap_cores(plane)
    params = place(core, plane, None, "place_mine")
    params = place(1 - core, other, params, "place_theirs").reshape(2, DIN, HEAD)
    return (params, new_master, new_moment, new_heads[0, :1], new_neurons.reshape(HEAD))


def solution(mesh):
    split = Mesh(mesh.devices.reshape(NZ, NY, NC, NX), ("z", "y", "c", "x"))
    return jax.shard_map(
        on_device,
        mesh=split,
        in_specs=(
            P(DP, None, None, "x"),
            P(None, DP, "x"),
            P(None, DP, "x"),
            P("x"),
            P("x"),
        ),
        out_specs=(
            P(None, None, "x"),
            P(None, DP, "x"),
            P(None, DP, "x"),
            P("x"),
            P("x"),
        ),
        check_vma=False,
    )
```

time: 139 us -> 137 us (0.986)
  blocking collectives: 50.8 us -> 75.2 us
  waiting for transfers between devices: 31 us -> 13.1 us
  starting transfers between devices: 37 us -> 31.2 us
  other arithmetic: 7.37 us -> 5.85 us
    all_to_all x2 -> x3, blocking collectives: 50.8 us -> 75.2 us  [exchange(): lax.all_to_all(blocks, axes, split_axis=0, concat_axis=0, tiled=True, axi...]
    all_to_all x2 -> x1, waiting for transfers between devices: 25.7 us -> 12 us  [exchange(): lax.all_to_all(blocks, axes, split_axis=0, concat_axis=0, tiled=True, axi...]
    ppermute x3 -> x2, starting transfers between devices: 25.7 us -> 19.9 us  [swap_cores(): return lax.ppermute(x, 'c', [(0, 1), (1, 0)])]
    ppermute x3 -> x2, waiting for transfers between devices: 5.21 us -> 1.13 us  [swap_cores(): return lax.ppermute(x, 'c', [(0, 1), (1, 0)])]
    pallas_call x3 -> x4, Pallas kernels: 3.94 us -> 4.38 us  [the longest x2 2.21 us: place(): pl.pallas_call(place_kernel, in_specs=[SMEM, VMEM] + [HBM] * len(before),...]
    all_to_all x2 -> x1, starting transfers between devices: 11.3 us -> 11.3 us  [exchange(): lax.all_to_all(blocks, axes, split_axis=0, concat_axis=0, tiled=True, axi...]
  transfers between devices with their start and end apart: 5 -> 3, of which waited for: 5 -> 2; matrix products, arithmetic and copies ran while one was open for 1% -> 1% of each run, Pallas kernels for 0% -> 1%
where the time goes in v4:
time: 137 us
  blocking collectives  75.2 us (55%)
  starting transfers between devices  31.2 us (23%)
  waiting for transfers between devices  13.1 us (10%)
  other arithmetic  5.85 us (4%)
  between operations  4.49 us (3%)
  Pallas kernels  4.38 us (3%)
  local copies, waits for them, and re-layouts  2.48 us (2%)
    all_to_all x3, blocking collectives, exchange(): lax.all_to_all(blocks, axes, split_axis=0, concat_axis=0, tiled=True, axi...  75.2 us
    ppermute x2, starting transfers between devices, swap_cores(): return lax.ppermute(x, 'c', [(0, 1), (1, 0)])  19.9 us
    all_to_all x1, waiting for transfers between devices, exchange(): lax.all_to_all(blocks, axes, split_axis=0, concat_axis=0, tiled=True, axi...  12 us
    all_to_all x1, starting transfers between devices, exchange(): lax.all_to_all(blocks, axes, split_axis=0, concat_axis=0, tiled=True, axi...  11.3 us
    reduce_max x4, other arithmetic, power_of(): jnp.max(jnp.abs(values))  4.01 us
  transfers between devices with their start and end apart: 3, of which 2 were waited for; matrix products, arithmetic and copies ran while one was open for 1% of the time, Pallas kernels for 1%

profile of v4, /device:TPU:1, one launch (start us, length us, event | category | flops | bytes accessed | tf_op | source)
XLA Modules:
  0.0 136.7 jit_solution(15532552488158233347)
XLA Ops:
  0.6 0.0 copy-start
  0.6 0.0 copy-start.1
  0.7 1.3 dynamic-slice_bitcast_fusion
  2.0 16.0 %collective-permute-start = (bf16[2,64,32,128]{3,2,1,0:T(8,128)(2,1)S(1)}, bf16[2,64,32,128]{3,2,1,0:T(8,128)(2,1)S(1)}, u32[]{:S(2)}, u32[]{:S(2)}) collective-permute-start(bf16[2,64,32,128]{3,2,1,0:T(8,128)(2,1)S(1)} %dynamic-slice_bitcast_fusion), channel_id=1, source_target_pairs={{0,8},{8,0},{1,9},{9,1},{2,10},{10,2},{3,11},{11,3},{4,12},{12,4},... | collective-permute-start | bytes 3145736 | tf_op jit(solution)/shard_map/ppermute | solution.py:46
  18.7 0.0 copy-done
  18.7 0.6 abs_reduce_fusion.2
  20.0 0.0 copy-done.1
  20.0 0.6 abs_reduce_fusion.3
  21.4 0.1 pad_add_fusion.where_ref
  21.6 0.0 collective-permute-done
  21.6 2.2 %abs_reduce_fusion = (f32[]{:T(128)}, f32[2,64,32,128]{3,2,1,0:T(8,128)S(1)}) fusion(bf16[2,64,32,128]{3,2,1,0:T(8,128)(2,1)S(1)} %collective-permute-done, bf16[2,64,2,32,128]{4,3,2,1,0:T(8,128)(2,1)} %bitcast.59, s32[]{:T(128)S(6)} %select_n.39), kind=kLoop, calls=%fused_computation.6 | loop fusion | flops 2621439 | bytes 4194312 | tf_op jit(solution)/shard_map/reduce_max | solution.py:50
  24.5 0.5 fusion.1
  25.0 0.3 copy.20
  25.3 0.3 pad_maximum_fusion
  25.7 20.4 %all_to_all.20 = f16[8,520,128]{2,1,0:T(8,128)(2,1)S(1)} all-to-all(f16[8,520,128]{2,1,0:T(8,128)(2,1)S(1)} %pad_maximum_fusion), channel_id=1, replica_groups={{0,128,256,384,512,640,768,896},{16,144,272,400,528,656,784,912},{32,16..., dimensions={0} | all-to-all | bytes 2129920 | tf_op jit(solution)/shard_map/all_to_all | solution.py:42
  46.0 0.1 copy.25
  46.1 0.3 multiply_reduce_fusion.1
  46.4 0.6 abs_reduce_fusion.1
  47.8 0.1 pad_maximum_fusion.1
  47.9 0.2 broadcast_in_dim.47
  48.1 31.8 %all_to_all.21 = f16[8,776,128]{2,1,0:T(8,128)(2,1)S(1)} all-to-all(f16[8,776,128]{2,1,0:T(8,128)(2,1)S(1)} %broadcast_in_dim.47), channel_id=1, replica_groups={{0,16,32,48,64,80,96,112},{128,144,160,176,192,208,224,240},{256,272,28..., dimensions={0} | all-to-all | bytes 3178496 | tf_op jit(solution)/shard_map/all_to_all | solution.py:42
  79.9 0.0 copy-start.2
  79.9 0.1 fusion.8
  80.0 0.1 copy.28
  80.1 0.1 copy.27
  80.2 0.1 copy.26
  80.3 0.3 multiply_reduce_fusion
  80.7 0.8 line_stats.1
  81.5 11.3 %all-to-all-start.2 = ((f32[128,2,128]{2,1,0:T(2,128)}), f32[128,2,128]{2,1,0:T(2,128)S(1)}, u32[]{:S(2)}, u32[]{:S(2)}) async-start(f32[128,2,128]{2,1,0:T(2,128)} %line_stats.1), calls=%async_computation.2 | async-start | bytes 262144 | tf_op jit(solution)/shard_map/all_to_all | solution.py:42
  92.8 0.1 add_multiply_fusion
  92.9 12.0 %all-to-all-done.2 = f32[128,2,128]{2,1,0:T(2,128)S(1)} async-done(((f32[128,2,128]{2,1,0:T(2,128)}), f32[128,2,128]{2,1,0:T(2,128)S(1)}, u32[]{:S(2)}, u32[]{:S(2)}) %all-to-all-start.2) | async-done | bytes 131104 | tf_op jit(solution)/shard_map/all_to_all | solution.py:42
  104.9 0.0 copy-done.2
  104.9 1.4 %update.1 = (bf16[8,2,32,128]{3,2,1,0:T(8,128)(2,1)S(1)}, f32[2,32,128]{2,1,0:T(8,128)}, f32[2,32,128]{2,1,0:T(8,128)}, f32[1,128]{1,0:T(1,128)}, f32[1,128]{1,0:T(1,128)}) custom-call(s32[2]{0:T(128)S(1)} %pad_add_fusion.where_ref, f32[16,8,2,128]{3,2,1,0:T(2,128)S(1)} %bitcast.51, f32[8,2,32,128]{3,2,1,0:T(8,128)S(1)} %bitcast.48, ...), custom_call_target="tpu_custom_call" | custom-call | tf_op jit(solution)/shard_map/update/pallas_call | solution.py:128
  106.2 0.1 broadcast_in_dim.48
  106.4 23.1 %all_to_all.22 = bf16[8,512,128]{2,1,0:T(8,128)(2,1)S(1)} all-to-all(bf16[8,512,128]{2,1,0:T(8,128)(2,1)S(1)} %broadcast_in_dim.48), channel_id=1, replica_groups={{0,128,256,384,512,640,768,896},{16,144,272,400,528,656,784,912},{32,16..., dimensions={0} | all-to-all | bytes 2097152 | tf_op jit(solution)/shard_map/all_to_all | solution.py:42
  129.5 3.9 %collective-permute-start.1 = (bf16[8,8,2,32,128]{4,3,2,1,0:T(8,128)(2,1)S(1)}, bf16[8,8,2,32,128]{4,3,2,1,0:T(8,128)(2,1)S(1)}, u32[]{:S(2)}, u32[]{:S(2)}) collective-permute-start(bf16[8,8,2,32,128]{4,3,2,1,0:T(8,128)(2,1)S(1)} %bitcast.45), channel_id=1, source_target_pairs={{0,8},{8,0},{1,9},{9,1},{2,10},{10,2},{3,11},{11,3},{4,12},{12,4},... | collective-permute-start | bytes 3145736 | tf_op jit(solution)/shard_map/ppermute | solution.py:46
  133.4 1.1 place_mine.1.rest_0_
  134.5 1.1 collective-permute-done.1.plane_ref
  135.7 1.1 place_theirs.1
  (17 shorter events, 0.2 us)
Async XLA Ops:
  0.6 18.0 %copy-start = (f32[2,32,128]{2,1,0:T(8,128)S(1)}, f32[2,32,128]{2,1,0:T(8,128)}, u32[]{:S(2)}) copy-start(f32[2,32,128]{2,1,0:T(8,128)} %own_moment_ref.1) | copy-start | bytes 98308
  0.6 19.4 %copy-start.1 = (f32[2,32,128]{2,1,0:T(8,128)S(1)}, f32[2,32,128]{2,1,0:T(8,128)}, u32[]{:S(2)}) copy-start(f32[2,32,128]{2,1,0:T(8,128)} %own_master_ref.1) | copy-start | bytes 98308
  2.0 19.6 %collective-permute-start = (bf16[2,64,32,128]{3,2,1,0:T(8,128)(2,1)S(1)}, bf16[2,64,32,128]{3,2,1,0:T(8,128)(2,1)S(1)}, u32[]{:S(2)}, u32[]{:S(2)}) collective-permute-start(bf16[2,64,32,128]{3,2,1,0:T(8,128)(2,1)S(1)} %dynamic-slice_bitcast_fusion), channel_id=1, source_target_pairs={{0,8},{8,0},{1,9},{9,1},{2,10},{10,2},{3,11},{11,3},{4,12},{12,4},... | collective-permute-start | bytes 3145736 | tf_op jit(solution)/shard_map/ppermute | solution.py:46
  79.9 24.9 %copy-start.2 = (f32[128]{0:T(128)S(1)}, f32[128]{0:T(128)}, u32[]{:S(2)}) copy-start(f32[128]{0:T(128)} %param.9) | copy-start | bytes 1540
  81.5 23.4 %all-to-all-start.2 = ((f32[128,2,128]{2,1,0:T(2,128)}), f32[128,2,128]{2,1,0:T(2,128)S(1)}, u32[]{:S(2)}, u32[]{:S(2)}) async-start(f32[128,2,128]{2,1,0:T(2,128)} %line_stats.1), calls=%async_computation.2 | async-start | bytes 262144 | tf_op jit(solution)/shard_map/all_to_all | solution.py:42
  129.5 6.2 %collective-permute-start.1 = (bf16[8,8,2,32,128]{4,3,2,1,0:T(8,128)(2,1)S(1)}, bf16[8,8,2,32,128]{4,3,2,1,0:T(8,128)(2,1)S(1)}, u32[]{:S(2)}, u32[]{:S(2)}) collective-permute-start(bf16[8,8,2,32,128]{4,3,2,1,0:T(8,128)(2,1)S(1)} %bitcast.45), channel_id=1, source_target_pairs={{0,8},{8,0},{1,9},{9,1},{2,10},{10,2},{3,11},{11,3},{4,12},{12,4},... | collective-permute-start | bytes 3145736 | tf_op jit(solution)/shard_map/ppermute | solution.py:46

commit v5 on v4

--- a/solution.py
+++ b/solution.py
@@ -46,8 +46,9 @@
     return lax.ppermute(x, "c", [(0, 1), (1, 0)])
 
 
-def power_of(values):
-    return jnp.floor(jnp.log2(jnp.maximum(jnp.max(jnp.abs(values)), 2.0**-100)))
+def power_of(values, axes):
+    largest = jnp.max(jnp.abs(values), axis=axes)
+    return jnp.floor(jnp.log2(jnp.maximum(largest, 2.0**-100)))
 
 
 def as_half(values, power):
@@ -61,17 +62,17 @@
     return [high.astype(jnp.float16).reshape(2 * ROWS, HEAD), low.astype(jnp.float16).reshape(2 * ROWS, HEAD)]
 
 
-def lane_row(k, power):
-    lane = lax.broadcasted_iota(jnp.int32, (8, HEAD), 1)
-    return jnp.where(lane == k, power, 0.0)
+def row_at(k, power):
+    row = lax.broadcasted_iota(jnp.int32, (8, HEAD), 0)
+    return jnp.where(row == k, power, 0.0)
 
 
 def out_of_two(high, low, scale):
-    return (high.astype(jnp.float32) + low.astype(jnp.float32) * (1.0 / LOW)) * scale[:, None, None]
-
-
-def scale_at(got, row, lane):
-    return jnp.exp2(got[:, row, lane].astype(jnp.float32) - 14.0)
+    return (high.astype(jnp.float32) + low.astype(jnp.float32) * (1.0 / LOW)) * scale[:, None, :]
+
+
+def scale_at(got, row):
+    return jnp.exp2(got[:, row].astype(jnp.float32) - 14.0)
 
 
 def line_stats_kernel(gradient_ref, out_ref):
@@ -180,33 +181,33 @@
     theirs = lax.dynamic_index_in_dim(halves, 1 - c, 2, keepdims=False)
     halves, theirs = lax.optimization_barrier((halves, theirs))
     mine = lax.dynamic_index_in_dim(halves, c, 2, keepdims=False)
-    power_a, power_o = power_of(master), power_of(moment)
+    power_a, power_o = power_of(master, (0, 1)), power_of(moment, (0, 1))
     state = jnp.concatenate(in_two(master, power_a) + in_two(moment, power_o), axis=0)
     heads = jnp.broadcast_to(v_heads, (1, HEAD))
     neurons = v_neurons.reshape(1, HEAD)
     sums = mine.astype(jnp.float32) + swap_cores(theirs).astype(jnp.float32)
-    power = power_of(sums)
+    power = power_of(sums, None)
     sums = sums.reshape(2, 8, 8, ROWS, HEAD)
     ordered = jnp.where(c == 0, sums.transpose(1, 2, 0, 3, 4), sums.transpose(2, 1, 0, 3, 4))
     message = jnp.concatenate(
-        [as_half(ordered, power).reshape(8, 512, HEAD), jnp.broadcast_to(lane_row(0, power).astype(jnp.float16), (8, 8, HEAD))], axis=1
-    )
-    first_lane, powers = lane_row(0, 1.0), lane_row(1, power_a) + lane_row(2, power_o)
-    message, state, first_lane, powers, where, core, heads = lax.optimization_barrier(
-        (message, state, first_lane, powers, where, core, heads)
+        [as_half(ordered, power).reshape(8, 512, HEAD), jnp.full((8, 8, HEAD), power, jnp.float16)], axis=1
+    )
+    first_row, powers = row_at(0, 1.0), row_at(1, power_a) + row_at(2, power_o)
+    message, state, first_row, powers, where, core, heads = lax.optimization_barrier(
+        (message, state, first_row, powers, where, core, heads)
     )
     got = exchange(message, DP, FIRST)
-    partial = jnp.sum(got[:, :512].astype(jnp.float32) * scale_at(got, 512, 0)[:, None, None], axis=0)
-
-    power = power_of(partial)
-    message = jnp.concatenate([as_half(partial, power), state, (powers + power * first_lane).astype(jnp.float16)], axis=0)
+    partial = jnp.sum(got[:, :512].astype(jnp.float32) * scale_at(got, 512)[:, None, :], axis=0)
+
+    power = power_of(partial, 0)
+    message = jnp.concatenate([as_half(partial, power), state, (powers + power * first_row).astype(jnp.float16)], axis=0)
     message = lax.optimization_barrier(message)
     got = exchange(jnp.broadcast_to(message, (8, *message.shape)), DP, SECOND)
-    gradient = jnp.sum(got[:, :512].astype(jnp.float32) * scale_at(got, 768, 0)[:, None, None], axis=0) / 128.0
+    gradient = jnp.sum(got[:, :512].astype(jnp.float32) * scale_at(got, 768)[:, None, :], axis=0) / 128.0
     gradient = gradient.reshape(8, 2, ROWS, HEAD)
     stats = exchange(line_stats(gradient), (*DP, "x"), STATS)
-    line_master = out_of_two(got[:, 512:576], got[:, 576:640], scale_at(got, 768, 1)).reshape(8, 2, ROWS, HEAD)
-    line_moment = out_of_two(got[:, 640:704], got[:, 704:768], scale_at(got, 768, 2)).reshape(8, 2, ROWS, HEAD)
+    line_master = out_of_two(got[:, 512:576], got[:, 576:640], scale_at(got, 769)).reshape(8, 2, ROWS, HEAD)
+    line_moment = out_of_two(got[:, 640:704], got[:, 704:768], scale_at(got, 770)).reshape(8, 2, ROWS, HEAD)
     params, new_master, new_moment, new_heads, new_neurons = update_of(
         where, stats.reshape(16, NX, 2, HEAD), gradient, line_master, line_moment, master, moment, heads, neurons
     )

time: 137 us -> 134 us (0.978)
  between operations: 4.49 us -> 2.27 us
  other arithmetic: 5.85 us -> 3.76 us
    reduce_max x4, other arithmetic: 4.01 us -> 2.25 us  [power_of(): largest = jnp.max(jnp.abs(values), axis=axes)]
  transfers between devices with their start and end apart: 3 -> 3, of which waited for: 2 -> 3; matrix products, arithmetic and copies ran while one was open for 1% -> 0% of each run, Pallas kernels for 1% -> 1%
where the time goes in v5:
time: 134 us
  blocking collectives  75.2 us (56%)
  starting transfers between devices  31.6 us (24%)
  waiting for transfers between devices  14.3 us (11%)
  Pallas kernels  4.38 us (3%)
  other arithmetic  3.76 us (3%)
  local copies, waits for them, and re-layouts  2.27 us (2%)
  between operations  2.27 us (2%)
    all_to_all x3, blocking collectives, exchange(): lax.all_to_all(blocks, axes, split_axis=0, concat_axis=0, tiled=True, axi...  75.2 us
    ppermute x2, starting transfers between devices, swap_cores(): return lax.ppermute(x, 'c', [(0, 1), (1, 0)])  19.9 us
    all_to_all x1, waiting for transfers between devices, exchange(): lax.all_to_all(blocks, axes, split_axis=0, concat_axis=0, tiled=True, axi...  12 us
    all_to_all x1, starting transfers between devices, exchange(): lax.all_to_all(blocks, axes, split_axis=0, concat_axis=0, tiled=True, axi...  11.6 us
  transfers between devices with their start and end apart: 3, of which 3 were waited for; matrix products, arithmetic and copies ran while one was open for 0% of the time, Pallas kernels for 1%

profile of v5, /device:TPU:1, one launch (start us, length us, event | category | flops | bytes accessed | tf_op | source)
XLA Modules:
  0.0 133.8 jit_solution(9065601419752041682)
XLA Ops:
  0.6 0.0 copy-start.1
  0.6 0.0 copy-start
  0.7 1.3 dynamic-slice_bitcast_fusion
  2.0 16.0 %collective-permute-start = (bf16[2,64,32,128]{3,2,1,0:T(8,128)(2,1)S(1)}, bf16[2,64,32,128]{3,2,1,0:T(8,128)(2,1)S(1)}, u32[]{:S(2)}, u32[]{:S(2)}) collective-permute-start(bf16[2,64,32,128]{3,2,1,0:T(8,128)(2,1)S(1)} %dynamic-slice_bitcast_fusion), channel_id=1, source_target_pairs={{0,8},{8,0},{1,9},{9,1},{2,10},{10,2},{3,11},{11,3},{4,12},{12,4},... | collective-permute-start | bytes 3145736 | tf_op jit(solution)/shard_map/ppermute | solution.py:46
  18.0 0.0 copy-done.1
  18.1 0.0 copy-done
  18.1 0.1 pad_add_fusion.where_ref
  19.0 0.1 select_add_fusion
  19.0 1.2 collective-permute-done
  20.3 2.2 %abs_reduce_fusion = (f32[]{:T(128)}, f32[2,64,32,128]{3,2,1,0:T(8,128)S(1)}) fusion(bf16[2,64,32,128]{3,2,1,0:T(8,128)(2,1)S(1)} %collective-permute-done, bf16[2,64,2,32,128]{4,3,2,1,0:T(8,128)(2,1)} %bitcast.59, s32[]{:T(128)S(6)} %select_n.33), kind=kLoop, calls=%fused_computation.6 | loop fusion | flops 2621439 | bytes 4194312 | tf_op jit(solution)/shard_map/reduce_max | solution.py:50
  23.2 0.5 fusion.1
  23.7 0.3 copy.30
  24.0 0.2 concatenate.9
  24.2 0.1 iota.19
  24.3 20.3 %all_to_all.20 = f16[8,520,128]{2,1,0:T(8,128)(2,1)S(1)} all-to-all(f16[8,520,128]{2,1,0:T(8,128)(2,1)S(1)} %concatenate.9), channel_id=1, replica_groups={{0,128,256,384,512,640,768,896},{16,144,272,400,528,656,784,912},{32,16..., dimensions={0} | all-to-all | bytes 2129920 | tf_op jit(solution)/shard_map/all_to_all | solution.py:42
  44.7 0.2 multiply_reduce_fusion.1
  45.0 0.1 pad_maximum_fusion
  45.1 0.2 broadcast_in_dim.46
  45.3 31.8 %all_to_all.21 = f16[8,776,128]{2,1,0:T(8,128)(2,1)S(1)} all-to-all(f16[8,776,128]{2,1,0:T(8,128)(2,1)S(1)} %broadcast_in_dim.46), channel_id=1, replica_groups={{0,16,32,48,64,80,96,112},{128,144,160,176,192,208,224,240},{256,272,28..., dimensions={0} | all-to-all | bytes 3178496 | tf_op jit(solution)/shard_map/all_to_all | solution.py:42
  77.1 0.0 copy-start.2
  77.1 0.2 multiply_reduce_fusion
  77.4 0.8 line_stats.1
  78.2 11.6 %all-to-all-start.2 = ((f32[128,2,128]{2,1,0:T(2,128)}), f32[128,2,128]{2,1,0:T(2,128)S(1)}, u32[]{:S(2)}, u32[]{:S(2)}) async-start(f32[128,2,128]{2,1,0:T(2,128)} %line_stats.1), calls=%async_computation.2 | async-start | bytes 262144 | tf_op jit(solution)/shard_map/all_to_all | solution.py:42
  89.9 0.1 add_multiply_fusion
  90.0 12.0 %all-to-all-done.2 = f32[128,2,128]{2,1,0:T(2,128)S(1)} async-done(((f32[128,2,128]{2,1,0:T(2,128)}), f32[128,2,128]{2,1,0:T(2,128)S(1)}, u32[]{:S(2)}, u32[]{:S(2)}) %all-to-all-start.2) | async-done | bytes 131104 | tf_op jit(solution)/shard_map/all_to_all | solution.py:42
  101.9 0.0 copy-done.2
  101.9 1.4 %update.1 = (bf16[8,2,32,128]{3,2,1,0:T(8,128)(2,1)S(1)}, f32[2,32,128]{2,1,0:T(8,128)}, f32[2,32,128]{2,1,0:T(8,128)}, f32[1,128]{1,0:T(1,128)}, f32[1,128]{1,0:T(1,128)}) custom-call(s32[2]{0:T(128)S(1)} %pad_add_fusion.where_ref, f32[16,8,2,128]{3,2,1,0:T(2,128)S(1)} %bitcast.51, f32[8,2,32,128]{3,2,1,0:T(8,128)S(1)} %bitcast.48, ...), custom_call_target="tpu_custom_call" | custom-call | tf_op jit(solution)/shard_map/update/pallas_call | solution.py:129
  103.3 0.1 broadcast_in_dim.47
  103.5 23.1 %all_to_all.22 = bf16[8,512,128]{2,1,0:T(8,128)(2,1)S(1)} all-to-all(bf16[8,512,128]{2,1,0:T(8,128)(2,1)S(1)} %broadcast_in_dim.47), channel_id=1, replica_groups={{0,128,256,384,512,640,768,896},{16,144,272,400,528,656,784,912},{32,16..., dimensions={0} | all-to-all | bytes 2097152 | tf_op jit(solution)/shard_map/all_to_all | solution.py:42
  126.5 3.9 %collective-permute-start.1 = (bf16[8,8,2,32,128]{4,3,2,1,0:T(8,128)(2,1)S(1)}, bf16[8,8,2,32,128]{4,3,2,1,0:T(8,128)(2,1)S(1)}, u32[]{:S(2)}, u32[]{:S(2)}) collective-permute-start(bf16[8,8,2,32,128]{4,3,2,1,0:T(8,128)(2,1)S(1)} %bitcast.45), channel_id=1, source_target_pairs={{0,8},{8,0},{1,9},{9,1},{2,10},{10,2},{3,11},{11,3},{4,12},{12,4},... | collective-permute-start | bytes 3145736 | tf_op jit(solution)/shard_map/ppermute | solution.py:46
  130.5 1.1 place_mine.1.rest_0_
  131.6 1.1 collective-permute-done.1.plane_ref
  132.7 1.1 place_theirs.1
  (20 shorter events, 0.3 us)
Async XLA Ops:
  0.6 17.4 %copy-start.1 = (f32[2,32,128]{2,1,0:T(8,128)S(1)}, f32[2,32,128]{2,1,0:T(8,128)}, u32[]{:S(2)}) copy-start(f32[2,32,128]{2,1,0:T(8,128)} %own_master_ref.1) | copy-start | bytes 98308
  0.6 17.4 %copy-start = (f32[2,32,128]{2,1,0:T(8,128)S(1)}, f32[2,32,128]{2,1,0:T(8,128)}, u32[]{:S(2)}) copy-start(f32[2,32,128]{2,1,0:T(8,128)} %own_moment_ref.1) | copy-start | bytes 98308
  2.0 18.3 %collective-permute-start = (bf16[2,64,32,128]{3,2,1,0:T(8,128)(2,1)S(1)}, bf16[2,64,32,128]{3,2,1,0:T(8,128)(2,1)S(1)}, u32[]{:S(2)}, u32[]{:S(2)}) collective-permute-start(bf16[2,64,32,128]{3,2,1,0:T(8,128)(2,1)S(1)} %dynamic-slice_bitcast_fusion), channel_id=1, source_target_pairs={{0,8},{8,0},{1,9},{9,1},{2,10},{10,2},{3,11},{11,3},{4,12},{12,4},... | collective-permute-start | bytes 3145736 | tf_op jit(solution)/shard_map/ppermute | solution.py:46
  77.1 24.8 %copy-start.2 = (f32[128]{0:T(128)S(1)}, f32[128]{0:T(128)}, u32[]{:S(2)}) copy-start(f32[128]{0:T(128)} %param.9) | copy-start | bytes 1540
  78.2 23.8 %all-to-all-start.2 = ((f32[128,2,128]{2,1,0:T(2,128)}), f32[128,2,128]{2,1,0:T(2,128)S(1)}, u32[]{:S(2)}, u32[]{:S(2)}) async-start(f32[128,2,128]{2,1,0:T(2,128)} %line_stats.1), calls=%async_computation.2 | async-start | bytes 262144 | tf_op jit(solution)/shard_map/all_to_all | solution.py:42
  126.5 6.2 %collective-permute-start.1 = (bf16[8,8,2,32,128]{4,3,2,1,0:T(8,128)(2,1)S(1)}, bf16[8,8,2,32,128]{4,3,2,1,0:T(8,128)(2,1)S(1)}, u32[]{:S(2)}, u32[]{:S(2)}) collective-permute-start(bf16[8,8,2,32,128]{4,3,2,1,0:T(8,128)(2,1)S(1)} %bitcast.45), channel_id=1, source_target_pairs={{0,8},{8,0},{1,9},{9,1},{2,10},{10,2},{3,11},{11,3},{4,12},{12,4},... | collective-permute-start | bytes 3145736 | tf_op jit(solution)/shard_map/ppermute | solution.py:46

commit v6 on v5

--- a/solution.py
+++ b/solution.py
@@ -205,9 +205,10 @@
     got = exchange(jnp.broadcast_to(message, (8, *message.shape)), DP, SECOND)
     gradient = jnp.sum(got[:, :512].astype(jnp.float32) * scale_at(got, 768)[:, None, :], axis=0) / 128.0
     gradient = gradient.reshape(8, 2, ROWS, HEAD)
-    stats = exchange(line_stats(gradient), (*DP, "x"), STATS)
     line_master = out_of_two(got[:, 512:576], got[:, 576:640], scale_at(got, 769)).reshape(8, 2, ROWS, HEAD)
     line_moment = out_of_two(got[:, 640:704], got[:, 704:768], scale_at(got, 770)).reshape(8, 2, ROWS, HEAD)
+    stats, line_master, line_moment = lax.optimization_barrier((line_stats(gradient), line_master, line_moment))
+    stats = exchange(stats, (*DP, "x"), STATS)
     params, new_master, new_moment, new_heads, new_neurons = update_of(
         where, stats.reshape(16, NX, 2, HEAD), gradient, line_master, line_moment, master, moment, heads, neurons
     )

time: 134 us -> 134 us (level)
  blocking collectives: 75.2 us -> 98.8 us
  waiting for transfers between devices: 14.3 us -> 2.36 us
  starting transfers between devices: 31.6 us -> 19.9 us
    all_to_all x3 -> x4, blocking collectives: 75.2 us -> 98.8 us  [exchange(): lax.all_to_all(blocks, axes, split_axis=0, concat_axis=0, tiled=True, axi...]
    all_to_all x1 -> x0, waiting for transfers between devices: 12 us -> none  [exchange(): lax.all_to_all(blocks, axes, split_axis=0, concat_axis=0, tiled=True, axi...]
    all_to_all x1 -> x0, starting transfers between devices: 11.6 us -> none  [exchange(): lax.all_to_all(blocks, axes, split_axis=0, concat_axis=0, tiled=True, axi...]
  transfers between devices with their start and end apart: 3 -> 2, of which waited for: 3 -> 2; matrix products, arithmetic and copies ran while one was open for 0% -> 0% of each run, Pallas kernels for 1% -> 1%
where the time goes in v6:
time: 134 us; the launch traced here: 133 us
  blocking collectives  98.8 us (74%)
  starting transfers between devices  19.9 us (15%)
  other arithmetic  3.9 us (3%)
  Pallas kernels  3.73 us (3%)
  waiting for transfers between devices  2.36 us (2%)
  local copies, waits for them, and re-layouts  2.29 us (2%)
  between operations  2.26 us (2%)
    all_to_all x4, blocking collectives, exchange(): lax.all_to_all(blocks, axes, split_axis=0, concat_axis=0, tiled=True, axi...  98.8 us
    ppermute x2, starting transfers between devices, swap_cores(): return lax.ppermute(x, 'c', [(0, 1), (1, 0)])  19.9 us
  transfers between devices with their start and end apart: 2, of which 2 were waited for; matrix products, arithmetic and copies ran while one was open for 0% of the time, Pallas kernels for 1%

profile of v6, /device:TPU:1, one launch (start us, length us, event | category | flops | bytes accessed | tf_op | source)
XLA Modules:
  0.0 133.2 jit_solution(14078049331773338924)
XLA Ops:
  0.6 0.0 copy-start.1
  0.6 0.0 copy-start
  0.7 1.3 dynamic-slice_bitcast_fusion
  2.0 16.0 %collective-permute-start = (bf16[2,64,32,128]{3,2,1,0:T(8,128)(2,1)S(1)}, bf16[2,64,32,128]{3,2,1,0:T(8,128)(2,1)S(1)}, u32[]{:S(2)}, u32[]{:S(2)}) collective-permute-start(bf16[2,64,32,128]{3,2,1,0:T(8,128)(2,1)S(1)} %dynamic-slice_bitcast_fusion), channel_id=1, source_target_pairs={{0,8},{8,0},{1,9},{9,1},{2,10},{10,2},{3,11},{11,3},{4,12},{12,4},... | collective-permute-start | bytes 3145736 | tf_op jit(solution)/shard_map/ppermute | solution.py:46
  18.0 0.0 copy-done.1
  18.1 0.0 copy-done
  18.1 0.1 pad_add_fusion.where_ref
  19.0 0.1 select_add_fusion
  19.0 1.2 collective-permute-done
  20.3 2.3 %abs_reduce_fusion = (f32[]{:T(128)}, f32[2,64,32,128]{3,2,1,0:T(8,128)S(1)}) fusion(bf16[2,64,32,128]{3,2,1,0:T(8,128)(2,1)S(1)} %collective-permute-done, bf16[2,64,2,32,128]{4,3,2,1,0:T(8,128)(2,1)} %bitcast.59, s32[]{:T(128)S(6)} %select_n.33), kind=kLoop, calls=%fused_computation.6 | loop fusion | flops 2621439 | bytes 4194312 | tf_op jit(solution)/shard_map/reduce_max | solution.py:50
  23.3 0.5 fusion.1
  23.9 0.3 copy.30
  24.2 0.2 concatenate.9
  24.4 0.1 iota.19
  24.5 20.3 %all_to_all.20 = f16[8,520,128]{2,1,0:T(8,128)(2,1)S(1)} all-to-all(f16[8,520,128]{2,1,0:T(8,128)(2,1)S(1)} %concatenate.9), channel_id=1, replica_groups={{0,128,256,384,512,640,768,896},{16,144,272,400,528,656,784,912},{32,16..., dimensions={0} | all-to-all | bytes 2129920 | tf_op jit(solution)/shard_map/all_to_all | solution.py:42
  44.8 0.2 multiply_reduce_fusion.1
  45.2 0.1 pad_maximum_fusion
  45.2 0.2 broadcast_in_dim.46
  45.5 31.8 %all_to_all.21 = f16[8,776,128]{2,1,0:T(8,128)(2,1)S(1)} all-to-all(f16[8,776,128]{2,1,0:T(8,128)(2,1)S(1)} %broadcast_in_dim.46), channel_id=1, replica_groups={{0,16,32,48,64,80,96,112},{128,144,160,176,192,208,224,240},{256,272,28..., dimensions={0} | all-to-all | bytes 3178496 | tf_op jit(solution)/shard_map/all_to_all | solution.py:42
  77.2 0.0 copy-start.2
  77.3 0.2 multiply_reduce_fusion
  77.6 0.1 line_stats.1
  77.7 0.1 add_multiply_fusion
  77.8 23.5 %all_to_all.22 = f32[128,2,128]{2,1,0:T(2,128)S(1)} all-to-all(f32[128,2,128]{2,1,0:T(2,128)S(1)} %line_stats.1), channel_id=1, replica_groups={{0,1,2,3,4,5,6,7,128,129,130,131,132,133,134,135,256,257,258,259,260,26..., dimensions={0} | all-to-all | bytes 262144 | tf_op jit(solution)/shard_map/all_to_all | solution.py:42
  101.3 0.0 copy-done.2
  101.3 1.4 %update.1 = (bf16[8,2,32,128]{3,2,1,0:T(8,128)(2,1)S(1)}, f32[2,32,128]{2,1,0:T(8,128)}, f32[2,32,128]{2,1,0:T(8,128)}, f32[1,128]{1,0:T(1,128)}, f32[1,128]{1,0:T(1,128)}) custom-call(s32[2]{0:T(128)S(1)} %pad_add_fusion.where_ref, f32[16,8,2,128]{3,2,1,0:T(2,128)S(1)} %bitcast.51, f32[8,2,32,128]{3,2,1,0:T(8,128)S(1)} %bitcast.48, ...), custom_call_target="tpu_custom_call" | custom-call | tf_op jit(solution)/shard_map/update/pallas_call | solution.py:129
  102.7 0.1 broadcast_in_dim.47
  102.9 23.1 %all_to_all.23 = bf16[8,512,128]{2,1,0:T(8,128)(2,1)S(1)} all-to-all(bf16[8,512,128]{2,1,0:T(8,128)(2,1)S(1)} %broadcast_in_dim.47), channel_id=1, replica_groups={{0,128,256,384,512,640,768,896},{16,144,272,400,528,656,784,912},{32,16..., dimensions={0} | all-to-all | bytes 2097152 | tf_op jit(solution)/shard_map/all_to_all | solution.py:42
  126.0 3.9 %collective-permute-start.1 = (bf16[8,8,2,32,128]{4,3,2,1,0:T(8,128)(2,1)S(1)}, bf16[8,8,2,32,128]{4,3,2,1,0:T(8,128)(2,1)S(1)}, u32[]{:S(2)}, u32[]{:S(2)}) collective-permute-start(bf16[8,8,2,32,128]{4,3,2,1,0:T(8,128)(2,1)S(1)} %bitcast.45), channel_id=1, source_target_pairs={{0,8},{8,0},{1,9},{9,1},{2,10},{10,2},{3,11},{11,3},{4,12},{12,4},... | collective-permute-start | bytes 3145736 | tf_op jit(solution)/shard_map/ppermute | solution.py:46
  129.9 1.1 place_mine.1.rest_0_
  131.0 1.1 collective-permute-done.1.plane_ref
  132.1 1.1 place_theirs.1
  (20 shorter events, 0.3 us)
Async XLA Ops:
  0.6 17.4 %copy-start.1 = (f32[2,32,128]{2,1,0:T(8,128)S(1)}, f32[2,32,128]{2,1,0:T(8,128)}, u32[]{:S(2)}) copy-start(f32[2,32,128]{2,1,0:T(8,128)} %own_master_ref.1) | copy-start | bytes 98308
  0.6 17.4 %copy-start = (f32[2,32,128]{2,1,0:T(8,128)S(1)}, f32[2,32,128]{2,1,0:T(8,128)}, u32[]{:S(2)}) copy-start(f32[2,32,128]{2,1,0:T(8,128)} %own_moment_ref.1) | copy-start | bytes 98308
  2.0 18.3 %collective-permute-start = (bf16[2,64,32,128]{3,2,1,0:T(8,128)(2,1)S(1)}, bf16[2,64,32,128]{3,2,1,0:T(8,128)(2,1)S(1)}, u32[]{:S(2)}, u32[]{:S(2)}) collective-permute-start(bf16[2,64,32,128]{3,2,1,0:T(8,128)(2,1)S(1)} %dynamic-slice_bitcast_fusion), channel_id=1, source_target_pairs={{0,8},{8,0},{1,9},{9,1},{2,10},{10,2},{3,11},{11,3},{4,12},{12,4},... | collective-permute-start | bytes 3145736 | tf_op jit(solution)/shard_map/ppermute | solution.py:46
  77.2 24.1 %copy-start.2 = (f32[128]{0:T(128)S(1)}, f32[128]{0:T(128)}, u32[]{:S(2)}) copy-start(f32[128]{0:T(128)} %param.9) | copy-start | bytes 1540
  126.0 6.2 %collective-permute-start.1 = (bf16[8,8,2,32,128]{4,3,2,1,0:T(8,128)(2,1)S(1)}, bf16[8,8,2,32,128]{4,3,2,1,0:T(8,128)(2,1)S(1)}, u32[]{:S(2)}, u32[]{:S(2)}) collective-permute-start(bf16[8,8,2,32,128]{4,3,2,1,0:T(8,128)(2,1)S(1)} %bitcast.45), channel_id=1, source_target_pairs={{0,8},{8,0},{1,9},{9,1},{2,10},{10,2},{3,11},{11,3},{4,12},{12,4},... | collective-permute-start | bytes 3145736 | tf_op jit(solution)/shard_map/ppermute | solution.py:46
